TPU v7x, 32 devices: a whole 2x2x4 slice. The times are simulated.
32 devices in a mesh: dp: 8 (over y, x, core), seq: 4 (over z).
Axes of the slice: x: 2, y: 2, z: 4, core: 2. Of those that a mesh axis runs over, the one named last changes fastest.
Arguments:
- queries: bfloat16 [8, 1024, 2048], P('dp', 'seq'), may hold values from -6 to 6
- keys: bfloat16 [8, 1024, 1024], P('dp', 'seq'), may hold values from -6 to 6
- values: bfloat16 [8, 1024, 1024], P('dp', 'seq'), may hold values from -190 to 190
- segments: int32 [8, 1024], P('dp', 'seq'), may hold values from 0 to 2, never falling along the last dimension, each value on 1 to 640 neighbouring positions
- cotangent: bfloat16 [8, 1024, 2304], P('dp', 'seq'), may hold values from -6 to 6
- weight: float32 [2048, 2304], P(('dp', 'seq')), may hold values from -0.125 to 0.125
- first_moment: bfloat16 [2048, 2304], P(('dp', 'seq')), may hold values from -1 to 1
- first_scale: float32 [2048, 18], P(('dp', 'seq')), may hold values from 0.3 to 3
- second_moment: bfloat16 [2048, 2304], P(('dp', 'seq')), may hold values from 0.049804688 to 1
- second_scale: float32 [2048, 18], P(('dp', 'seq')), may hold values from 0.3 to 3
Outputs:
- layer_out: bfloat16 [8, 1024, 2304], P('dp', 'seq')
- new_weight: float32 [2048, 2304], P(('dp', 'seq'))
- new_first: bfloat16 [2048, 2304], P(('dp', 'seq'))
- new_first_scale: float32 [2048, 18], P(('dp', 'seq'))
- new_second: bfloat16 [2048, 2304], P(('dp', 'seq'))
- new_second_scale: float32 [2048, 18], P(('dp', 'seq'))
Inputs may be any that keep to these rules, and one draw needn't show every extreme that they name: `segments`: document numbers never fall along a sequence; each sequence holds 3 documents, one of exactly 640 positions.
All inputs are finite; a program needn't handle non-finite values. Where the computation divides by a largest or mean magnitude, that divisor is 1e-20 or more.
Results may differ from a plain program's by a relative error of at most 0.01.
Values may be sent and summed in bfloat16 or wider, within the bound.
A program may use at most 128 MiB of HBM per device.

v0:
```python
import functools

import jax
import jax.numpy as jnp
from jax import lax
from jax.experimental import pallas as pl
from jax.experimental.pallas import tpu as pltpu
from jax.sharding import PartitionSpec as P

HEADS = 16
KV_HEADS = 8
HEAD_DIM = 128
GROUP = 128

score_scale = 144.0 ** (-0.5)
soft_cap = 50.0
beta_first = 0.9
beta_second = 0.95
learn_rate = 0.001
decay_rate = 0.1

MESH = pl.DeviceIdType.MESH


def restore(blocks):
    grouped = blocks.astype(jnp.float32).reshape(blocks.shape[0], KV_HEADS, HEAD_DIM)
    scales = (jnp.max(jnp.abs(grouped), axis=-1) + 1e-06).astype(jnp.bfloat16)
    wide = scales.astype(jnp.float32)[..., None]
    coded = (grouped / wide).astype(jnp.bfloat16)
    return (coded.astype(jnp.float32) * wide).astype(jnp.bfloat16).reshape(blocks.shape)


def longest(length):
    return length * 5 // 8


def reach_skips(tokens, n):
    skips = []
    for s in range(1, n):
        skip = max(0, s * tokens - longest(n * tokens)) // 128 * 128
        if skip < tokens:
            skips.append(skip)
    return tuple(skips)


def orders(bits):
    high = list(range(1, bits))
    return (high, high[::-1])


def flip(me, r):
    out = me
    b = 0
    while (1 << b) <= r:
        if r & (1 << b):
            digit = lax.rem(lax.div(me, 1 << b), 2)
            out = out + (1 - 2 * digit) * (1 << b)
        b += 1
    return out


def gather_kernel(
    bits, n, skips,
    k_ref, v_ref, doc_ref, w_ref,
    k_all, v_all, doc_all, w_all,
    own_sem, ws, wr, ks, kr, ds_, dr, ts, tr,
):
    me = lax.axis_index("dp")
    z = lax.axis_index("seq")
    tokens = k_ref.shape[0]
    rows, width = w_ref.shape
    half = width // 2
    big = n * rows
    right, left = lax.rem(z + 1, n), lax.rem(z + n - 1, n)

    def w_slot(zz):
        start = pl.multiple_of((me * n + zz) * rows, 16)
        return w_all.at[pl.ds(start, rows), :]

    def kv_slot(ref, zz):
        return ref.at[pl.ds(pl.multiple_of(zz * tokens, 128), tokens), :]

    def doc_slot(zz):
        return doc_all.at[:, pl.ds(pl.multiple_of(zz * tokens, 128), tokens)]

    local = [
        pltpu.make_async_copy(k_ref, kv_slot(k_all, z), own_sem.at[0]),
        pltpu.make_async_copy(v_ref, kv_slot(v_all, z), own_sem.at[1]),
        pltpu.make_async_copy(doc_ref, doc_slot(z), own_sem.at[2]),
        pltpu.make_async_copy(w_ref, w_slot(z), own_sem.at[3]),
    ]
    for c in local:
        c.start()

    greet_bits(me, z, bits, n)

    started = []

    def remote(src, dst, ssem, rsem, dp, seq):
        copy = pltpu.make_async_remote_copy(
            src_ref=src, dst_ref=dst, send_sem=ssem, recv_sem=rsem,
            device_id={"dp": dp, "seq": seq}, device_id_type=MESH,
        )
        copy.start()
        started.append(copy)
        return copy

    def descriptor(src, dst, ssem, rsem, dp, seq):
        return pltpu.make_async_remote_copy(
            src_ref=src, dst_ref=dst, send_sem=ssem, recv_sem=rsem,
            device_id={"dp": dp, "seq": seq}, device_id_type=MESH,
        )

    def w_hop(direction, s):
        shift = n + 1 - s if direction == 0 else s - 1
        at = lax.rem(z + shift, n)
        here = w_ref if s == 1 else w_slot(at)
        return descriptor(
            here, w_slot(at), ws.at[direction, s - 1], wr.at[direction, s - 1],
            me, right if direction == 0 else left,
        )

    def kv_hop(part, s):
        at = lax.rem(z + n + 1 - s, n)
        ref = (k_ref, v_ref)[part]
        out = (k_all, v_all)[part]
        skip = skips[s - 1]
        start = pl.multiple_of(at * tokens + skip, 128)
        dst = out.at[pl.ds(start, tokens - skip), :]
        src = ref.at[pl.ds(skip, tokens - skip), :] if s == 1 else dst
        return descriptor(src, dst, ks.at[part, s - 1], kr.at[part, s - 1], me, right)

    def room(direction, s):
        if direction == 0:
            return (z >= s - 1) & (z < n - 1)
        return (z <= n - s) & (z > 0)

    def landed(direction, s):
        return z >= s if direction == 0 else z <= n - 1 - s

    steps = len(skips)
    for s in range(1, n):
        for direction in range(2):
            if s > 1:

                @pl.when(landed(direction, s - 1))
                def _(direction=direction, s=s):
                    w_hop(direction, s - 1).wait_recv()

            @pl.when(room(direction, s))
            def _(direction=direction, s=s):
                w_hop(direction, s).start()

    @pl.when(room(0, 1))
    def _():
        kv_hop(0, 1).start()
        kv_hop(1, 1).start()

    doc_copies = []
    for s in range(1, n):
        to = lax.rem(z + s, n)
        doc_copies.append(
            remote(doc_ref, doc_slot(z), ds_.at[s - 1], dr.at[s - 1], me, to)
        )
    for direction in range(2):

        @pl.when(landed(direction, n - 1))
        def _(direction=direction):
            w_hop(direction, n - 1).wait_recv()

    for c in local:
        c.wait()

    def kv_forward(s):
        for part in range(2):

            @pl.when(landed(0, s - 1))
            def _(part=part):
                kv_hop(part, s - 1).wait_recv()

            if s <= steps:

                @pl.when(room(0, s))
                def _(part=part):
                    kv_hop(part, s).start()

    tree = []
    for h, order in enumerate(orders(bits)):
        tree.append(list(order) + [0])

    def block(r, h):
        start = pl.multiple_of(flip(me, r) * big, 16)
        return w_all.at[pl.ds(start, big), pl.ds(h * half, half)]

    tc = {}

    def forward(r, h):
        order = tree[h]
        last = -1
        for i, b in enumerate(order):
            if r & (1 << b):
                last = i
        for b in order[last + 1:]:
            nr = r | (1 << b)
            tc[h, nr] = remote(
                block(r, h), block(r, h), ts.at[h, nr], tr.at[h, nr], flip(me, 1 << b), z
            )

    for h in range(2):
        forward(0, h)
    count = 1 << bits
    rank = []
    for h in range(2):
        seen = [0]
        for b in tree[h]:
            seen = seen + [r | (1 << b) for r in seen]
        rank.append(seen[1:])
    for i in range(count - 1):
        for h in range(2):
            r = rank[h][i]
            if r % 2 == 0:
                tc[h, r].wait_recv()
                forward(r, h)
        if i == 0 and steps >= 2:
            kv_forward(2)
        if i == count // 2 - 2:
            for s in range(3, steps + 1):
                kv_forward(s)
    kv_forward(steps + 1)
    for c in doc_copies:
        c.wait_recv()
    for i in range(count - 1):
        for h in range(2):
            r = rank[h][i]
            if r % 2 == 1:
                tc[h, r].wait_recv()
    for c in started:
        c.wait_send()
    for s in range(1, n):
        for direction in range(2):

            @pl.when(room(direction, s))
            def _(direction=direction, s=s):
                w_hop(direction, s).wait_send()

    for s in range(1, steps + 1):

        @pl.when(room(0, s))
        def _(s=s):
            kv_hop(0, s).wait_send()
            kv_hop(1, s).wait_send()


def greet_bits(me, z, bits, n):
    barrier = pltpu.get_barrier_semaphore()
    for b in range(bits):
        pl.semaphore_signal(
            barrier, inc=1, device_id={"dp": flip(me, 1 << b), "seq": z}, device_id_type=MESH
        )
    for s in range(1, n):
        pl.semaphore_signal(
            barrier, inc=1, device_id={"dp": me, "seq": lax.rem(z + s, n)}, device_id_type=MESH
        )
    pl.semaphore_wait(barrier, bits + n - 1)


def gather_all(k, v, docs, w, bits, n):
    tokens, kw = k.shape
    rows, width = w.shape
    skips = reach_skips(tokens, n)
    sem = pltpu.SemaphoreType.DMA
    vm = pl.BlockSpec(memory_space=pltpu.VMEM)
    hbm = pl.BlockSpec(memory_space=pl.ANY)
    count = 1 << bits
    return pl.pallas_call(
        functools.partial(gather_kernel, bits, n, skips),
        out_shape=(
            jax.ShapeDtypeStruct((n * tokens, kw), k.dtype),
            jax.ShapeDtypeStruct((n * tokens, kw), v.dtype),
            jax.ShapeDtypeStruct((8, n * tokens), docs.dtype),
            jax.ShapeDtypeStruct((count * n * rows, width), w.dtype),
        ),
        in_specs=[vm] * 4,
        out_specs=(hbm, hbm, hbm, hbm),
        scratch_shapes=[
            sem((4,)),
            sem((2, n - 1)), sem((2, n - 1)),
            sem((2, len(skips))), sem((2, len(skips))),
            sem((n - 1,)), sem((n - 1,)),
            sem((2, count)), sem((2, count)),
        ],
        compiler_params=pltpu.CompilerParams(collective_id=0, has_side_effects=True),
    )(k, v, docs, w)


def attend_kernel(q_ref, k_ref, v_ref, docs_ref, own_ref, o_ref):
    z = lax.axis_index("seq")
    tokens = q_ref.shape[0]
    length = k_ref.shape[0]
    key_at = lax.broadcasted_iota(jnp.int32, (tokens, length), 1)
    query_at = lax.broadcasted_iota(jnp.int32, (tokens, length), 0) + z * tokens
    allowed = (own_ref[:, 0:1] == docs_ref[0:1, :]) & (key_at <= query_at)
    place = lax.broadcasted_iota(jnp.int32, v_ref.shape, 0)
    seen = (place < (z + 1) * tokens) & (place >= z * tokens - longest(length))
    value = jnp.where(seen, v_ref[...].astype(jnp.float32), 0.0).astype(jnp.bfloat16)
    for i in range(2):
        cols = slice(i * HEAD_DIM, (i + 1) * HEAD_DIM)
        scores = lax.dot_general(
            q_ref[:, cols], k_ref[...], (((1,), (1,)), ((), ())),
            preferred_element_type=jnp.float32,
        )
        capped = soft_cap * jnp.tanh(scores * (score_scale / soft_cap))
        weights = jnp.where(allowed, jnp.exp(capped), 0.0)
        total = jnp.sum(weights, axis=-1, keepdims=True)
        mixed = jnp.dot(
            weights.astype(jnp.bfloat16), value, preferred_element_type=jnp.float32
        )
        o_ref[:, cols] = (mixed / total).astype(o_ref.dtype)


def attend(q, k_all, v_all, docs_all, own):
    tokens = q.shape[0]
    length = k_all.shape[0]
    pair = HEADS // KV_HEADS * HEAD_DIM
    return pl.pallas_call(
        attend_kernel,
        grid=(KV_HEADS,),
        out_shape=jax.ShapeDtypeStruct(q.shape, q.dtype),
        in_specs=[
            pl.BlockSpec((tokens, pair), lambda g: (0, g)),
            pl.BlockSpec((length, HEAD_DIM), lambda g: (0, g)),
            pl.BlockSpec((length, HEAD_DIM), lambda g: (0, g)),
            pl.BlockSpec((8, length), lambda g: (0, 0)),
            pl.BlockSpec((tokens, 128), lambda g: (0, 0)),
        ],
        out_specs=pl.BlockSpec((tokens, pair), lambda g: (0, g)),
    )(q, k_all, v_all, docs_all, own)


def step_kernel(
    bits, n,
    att_ref, cot_ref, own_ref, sum_ref,
    sb, rb, zs, zr, grad, tot_s, tot_r,
    bs, br, zss, zsr, qs, qr,
):
    me = lax.axis_index("dp")
    z = lax.axis_index("seq")
    rows, width = own_ref.shape
    half = width // 2
    big = n * rows
    count = 1 << bits
    right, left = lax.rem(z + 1, n), lax.rem(z + n - 1, n)
    started = []

    def remote(src, dst, ssem, rsem, dp, seq):
        copy = pltpu.make_async_remote_copy(
            src_ref=src, dst_ref=dst, send_sem=ssem, recv_sem=rsem,
            device_id={"dp": dp, "seq": seq}, device_id_type=MESH,
        )
        copy.start()
        started.append(copy)
        return copy

    greet_bits(me, z, bits, n)

    def product(r, h):
        start = pl.multiple_of(flip(me, r) * big, 128)
        return jnp.dot(
            att_ref[pl.ds(start, big), :],
            cot_ref[:, h * half:(h + 1) * half],
            preferred_element_type=jnp.float32,
        )

    tree = [[0] + list(order) for order in orders(bits)]
    sent = {}

    def first_bit(r, h):
        for b in tree[h]:
            if r & (1 << b):
                return b

    def push(r, h):
        b = first_bit(r, h)
        sent[h, r] = remote(
            sb.at[h, r], rb.at[h, r], bs.at[h, r], br.at[h, r], flip(me, 1 << b), z
        )

    seq_of = []
    for h in range(2):
        seen = [0]
        for b in tree[h][:0:-1]:
            seen = seen + [r | (1 << b) for r in seen]
        def key(r, h=h):
            if r == 0:
                return (len(tree[h]), 0)
            return (tree[h].index(first_bit(r, h)), r)
        seq_of.append(sorted(seen, key=key))
    for i in range(count // 2):
        for h in range(2):
            r = seq_of[h][i] | 1
            sb[h, r] = product(r, h).astype(jnp.bfloat16)
            push(r, h)
    for i in range(count // 2):
        for h in range(2):
            r = seq_of[h][i]
            value = product(r, h)
            for b in tree[h]:
                if r & (1 << b):
                    break
                src = r | (1 << b)
                sent[h, src].wait_recv()
                value = value + rb[h, src].astype(jnp.float32)
            if r:
                sb[h, r] = value.astype(jnp.bfloat16)
                push(r, h)
            else:
                grad[:, h * half:(h + 1) * half] = value

    def part(zz, h):
        start = pl.multiple_of(zz * rows, 16)
        return grad[pl.ds(start, rows), h * half:(h + 1) * half]

    ring = {}
    for s in range(n):
        for h in range(2):
            shift = (2 * n - 1 - s) if h == 0 else (1 + s)
            at = lax.rem(z + shift, n)
            value = part(at, h)
            if s:
                ring[h, s - 1].wait_recv()
                value = value + zr[h, s - 1].astype(jnp.float32)
            if s < n - 1:
                zs[h, s] = value.astype(jnp.bfloat16)
                ring[h, s] = remote(
                    zs.at[h, s], zr.at[h, s], zss.at[h, s], zsr.at[h, s],
                    me, right if h == 0 else left,
                )
            else:
                own_ref[:, h * half:(h + 1) * half] = value

    own = own_ref[...]
    total = jnp.broadcast_to(
        jnp.sum(jnp.sum(own * own, axis=1, keepdims=True), axis=0, keepdims=True), (8, 128)
    )
    for b in range(bits):
        tot_s[b] = total
        c = remote(tot_s.at[b], tot_r.at[b], qs.at[b], qr.at[b], flip(me, 1 << b), z)
        c.wait_recv()
        total = total + tot_r[b]
    tot_s[bits] = total
    last = []
    for s in range(1, n):
        i = bits + s - 1
        last.append(
            remote(tot_s.at[bits], tot_r.at[i], qs.at[i], qr.at[i], me, lax.rem(z + s, n))
        )
    for s in range(1, n):
        last[s - 1].wait_recv()
        total = total + tot_r[bits + s - 1]

    sum_ref[...] = total
    for c in started:
        c.wait_send()


def adam_kernel(
    entries,
    grad_ref, sum_ref, w_ref, m1_ref, s1_ref, m2_ref, s2_ref,
    nw_ref, n1_ref, ns1_ref, n2_ref, ns2_ref,
):
    width = w_ref.shape[1]
    rms = jnp.sqrt(sum_ref[0:1, :] / entries + 1e-06)
    factor = jnp.minimum(1.0, 1.0 / rms)

    def decode(coded, scale):
        x = coded.astype(jnp.float32)
        root = scale * jnp.sqrt(jnp.abs(x))
        return jnp.where(x < 0, -root, root)

    def encode(x):
        scale = jnp.max(jnp.abs(x), axis=-1, keepdims=True) + 1e-06
        return (x * jnp.abs(x) / (scale * scale)).astype(jnp.bfloat16), scale

    for g in range(width // GROUP):
        cols = slice(g * GROUP, (g + 1) * GROUP)
        clipped = grad_ref[:, cols] * factor
        first = beta_first * decode(m1_ref[:, cols], s1_ref[:, g:g + 1]) + (
            1.0 - beta_first
        ) * clipped
        second = (
            beta_second * decode(m2_ref[:, cols], s2_ref[:, g:g + 1])
            + (1.0 - beta_second) * clipped * clipped
        )
        weight = w_ref[:, cols]
        nw_ref[:, cols] = weight - learn_rate * (
            first / (jnp.sqrt(second) + 1e-08) + decay_rate * weight
        )
        n1_ref[:, cols], ns1_ref[:, g:g + 1] = encode(first)
        n2_ref[:, cols], ns2_ref[:, g:g + 1] = encode(second)


def train_step(att_t, cot, weight, m1, s1, m2, s2, bits, n):
    rows, width = weight.shape
    half = width // 2
    count = 1 << bits
    sem = pltpu.SemaphoreType.DMA
    vm = pl.BlockSpec(memory_space=pltpu.VMEM)
    like = lambda a: jax.ShapeDtypeStruct(a.shape, a.dtype)
    grad, total = pl.pallas_call(
        functools.partial(step_kernel, bits, n),
        out_shape=(like(weight), jax.ShapeDtypeStruct((8, 128), jnp.float32)),
        in_specs=[vm] * 2,
        out_specs=(vm,) * 2,
        scratch_shapes=[
            pltpu.VMEM((2, count, n * rows, half), jnp.bfloat16),
            pltpu.VMEM((2, count, n * rows, half), jnp.bfloat16),
            pltpu.VMEM((2, n - 1, rows, half), jnp.bfloat16),
            pltpu.VMEM((2, n - 1, rows, half), jnp.bfloat16),
            pltpu.VMEM((n * rows, width), jnp.float32),
            pltpu.VMEM((bits + 1, 8, 128), jnp.float32),
            pltpu.VMEM((bits + n - 1, 8, 128), jnp.float32),
            sem((2, count)), sem((2, count)),
            sem((2, n - 1)), sem((2, n - 1)),
            sem((bits + n - 1,)), sem((bits + n - 1,)),
        ],
        compiler_params=pltpu.CompilerParams(
            collective_id=1, has_side_effects=True, vmem_limit_bytes=60 * 1024 * 1024
        ),
    )(att_t, cot)
    return pl.pallas_call(
        functools.partial(adam_kernel, float(count * n * rows * width)),
        out_shape=(like(weight), like(m1), like(s1), like(m2), like(s2)),
        in_specs=[vm] * 7,
        out_specs=(vm,) * 5,
    )(grad, total, weight, m1, s1, m2, s2)


def local(
    bits, n,
    queries, keys, values, segments, cotangent, weight,
    first_moment, first_scale, second_moment, second_scale,
):
    docs = segments[0]
    tokens = docs.shape[0]
    k_all, v_all, docs_all, w_all = gather_all(
        restore(keys[0]),
        restore(values[0]),
        jnp.broadcast_to(docs[None, :], (8, tokens)),
        weight.astype(jnp.bfloat16),
        bits, n,
    )
    own = jnp.broadcast_to(docs[:, None], (tokens, 128))
    attended = attend(queries[0], k_all, v_all, docs_all, own)
    layer_out = jnp.dot(attended, w_all, preferred_element_type=jnp.float32)
    layer_out = layer_out.astype(jnp.bfloat16)[None]
    new_weight, new_first, new_first_scale, new_second, new_second_scale = train_step(
        attended.T, cotangent[0], weight, first_moment, first_scale,
        second_moment, second_scale, bits, n,
    )
    return (layer_out, new_weight, new_first, new_first_scale, new_second, new_second_scale)


def solution(mesh):
    bits = mesh.shape["dp"].bit_length() - 1
    n = mesh.shape["seq"]
    shard = P(("dp", "seq"), None)
    tok = P("dp", "seq", None)
    return jax.shard_map(
        functools.partial(local, bits, n),
        mesh=mesh,
        in_specs=(tok, tok, tok, P("dp", "seq"), tok, shard, shard, shard, shard, shard),
        out_specs=(tok, shard, shard, shard, shard, shard),
        check_vma=False,
    )
```

profile of v0, /device:TPU:0, one launch (start us, length us, event | category | flops | bytes accessed | tf_op | source)
XLA Modules:
  0.0 203.7 jit_solution(2353299450278209785)
XLA Ops:
  0.6 1.2 fusion.3
  1.8 0.0 copy-start.2
  1.8 0.2 copy.37
  2.0 0.3 reduce_max.18
  2.4 0.1 copy.28
  2.4 0.1 copy.29
  2.6 0.3 div.22
  2.9 0.0 copy-done.2
  2.9 0.1 fusion.6
  3.0 0.0 copy-start.3
  3.1 0.2 copy.39
  3.3 0.3 reduce_max.19
  3.6 0.1 copy.30
  3.7 0.1 copy.31
  3.8 0.3 div.25
  4.2 0.0 copy-start.6
  4.2 0.0 copy-start.1
  4.2 1.7 fusion.7
  5.9 0.0 copy-done.6
  5.9 0.6 broadcast_in_dim.18.doc_ref
  6.5 0.7 convert_element_type.104.w_ref
  7.2 70.6 %shard_map.145 = (bf16[1024,1024]{1,0:T(8,128)(2,1)}, bf16[1024,1024]{1,0:T(8,128)(2,1)}, s32[8,1024]{1,0:T(8,128)}, bf16[2048,2304]{1,0:T(8,128)(2,1)}) custom-call(bf16[256,1024]{1,0:T(8,128)(2,1)} %get-tuple-element.47.k_ref, bf16[256,1024]{1,0:T(8,128)(2,1)} %get-tuple-element.46.v_ref, s32[8,256]{1,0:T(8,128)} %broadcast_in_dim.18.doc_ref, ...), custom_call_target="tpu_custom_call" | custom-call | tf_op jit(solution)/shard_map/pallas_call | solution.py:275
  77.8 0.8 broadcast_in_dim.19.own_ref
  78.6 12.4 %shard_map.146 = bf16[256,2048]{1,0:T(8,128)(2,1)} custom-call(bf16[256,2048]{1,0:T(8,128)(2,1)} %bitcast.54, bf16[1024,1024]{1,0:T(8,128)(2,1)} %get-tuple-element.17.k_ref, bf16[1024,1024]{1,0:T(8,128)(2,1)} %get-tuple-element.18.v_ref, s32[8,1024]{1,0:T(8,128)} %get-tuple-element.19.docs_ref, s32[256,128]{1,0:T(8,128)} %broadcast_in_dim.19.own_ref), custom_call_target="tpu_custom_call" | custom-call | tf_op jit(solution)/shard_map/pallas_call | solution.py:325
  91.0 2.3 %copy.32 = bf16[256,2048]{0,1:T(8,128)(2,1)} copy(bf16[256,2048]{1,0:T(8,128)(2,1)} %shard_map.146) | data formatting | bytes 2097152 | tf_op jit(solution)/shard_map/pallas_call | solution.py:325
  93.3 94.5 %shard_map.147 = (f32[64,2304]{1,0:T(8,128)}, f32[8,128]{1,0:T(8,128)}) custom-call(bf16[2048,256]{1,0:T(8,128)(2,1)} %bitcast.49, bf16[256,2304]{1,0:T(8,128)(2,1)} %bitcast.53), custom_call_target="tpu_custom_call" | custom-call | tf_op jit(solution)/shard_map/pallas_call | solution.py:509
  187.7 0.7 copy.33.s1_ref
  188.4 0.7 copy.34.s2_ref
  189.1 4.4 %shard_map.148 = (f32[64,2304]{1,0:T(8,128)}, bf16[64,2304]{1,0:T(8,128)(2,1)}, f32[64,18]{1,0:T(8,128)}, bf16[64,2304]{1,0:T(8,128)(2,1)}, f32[64,18]{1,0:T(8,128)}) custom-call(f32[64,2304]{1,0:T(8,128)} %get-tuple-element.21.grad_ref, f32[8,128]{1,0:T(8,128)} %get-tuple-element.22.sum_ref, f32[64,2304]{1,0:T(8,128)} %w_ref.1, bf16[64,2304]{1,0:T(8,128)(2,1)} %m1_ref.1, ...), custom_call_target="tpu_custom_call" | custom-call | tf_op jit(solution)/shard_map/pallas_call | solution.py:530
  193.5 1.4 copy.35
  194.9 1.4 copy.36
  196.4 7.3 %fusion = bf16[1,256,2304]{2,1,0:T(8,128)(2,1)} fusion(bf16[256,2048]{1,0:T(8,128)(2,1)S(1)} %copy-done, bf16[2048,2304]{1,0:T(8,128)(2,1)} %get-tuple-element.20), kind=kOutput, calls=%fused_computation.1 | convolution fusion | flops 2416508928 | bytes 11665408 | tf_op jit(solution)/shard_map/dot_general | solution.py:554
  (10 shorter events, 0.0 us)
Async XLA Ops:
  1.8 1.1 copy-start.2
  3.0 1.1 copy-start.3
  4.2 1.7 copy-start.6
  4.2 2.3 %copy-start.1 = (f32[64,2304]{1,0:T(8,128)S(1)}, f32[64,2304]{1,0:T(8,128)}, u32[]{:S(2)}) copy-start(f32[64,2304]{1,0:T(8,128)} %w_ref.1) | copy-start | bytes 1769476
  91.0 96.7 %copy-start.4 = (f32[64,18]{0,1:T(8,128)S(1)}, f32[64,18]{0,1:T(8,128)}, u32[]{:S(2)}) copy-start(f32[64,18]{0,1:T(8,128)} %param.17) | copy-start | bytes 13828
  91.0 97.4 %copy-start.5 = (f32[64,18]{0,1:T(8,128)S(1)}, f32[64,18]{0,1:T(8,128)}, u32[]{:S(2)}) copy-start(f32[64,18]{0,1:T(8,128)} %param.19) | copy-start | bytes 13828
  93.3 103.1 %copy-start = (bf16[256,2048]{1,0:T(8,128)(2,1)S(1)}, bf16[256,2048]{1,0:T(8,128)(2,1)}, u32[]{:S(2)}) copy-start(bf16[256,2048]{1,0:T(8,128)(2,1)} %shard_map.146) | copy-start | bytes 3145732
where the time goes:
time: 204 us
  Pallas kernels  182 us (89%)
  local copies, waits for them, and re-layouts  9.37 us (5%)
  matrix products  7.29 us (4%)
  other arithmetic  4.38 us (2%)
    pallas_call x1, Pallas kernels, train_step(): pl.pallas_call(functools.partial(step_kernel, bits, n), out_shape=(like(w...  94.5 us
    pallas_call x1, Pallas kernels, gather_all(): pl.pallas_call(functools.partial(gather_kernel, bits, n, skips), out_shap...  70.6 us
    pallas_call x1, Pallas kernels, attend(): pl.pallas_call(attend_kernel, grid=(KV_HEADS,), out_shape=jax.ShapeDtypeS...  12.4 us
    dot_general x1, matrix products, local(): layer_out = jnp.dot(attended, w_all, preferred_element_type=jnp.float32)  7.29 us
    unnamed x20, local copies, waits for them, and re-layouts  4.69 us
    pallas_call x1, Pallas kernels, train_step(): pl.pallas_call(functools.partial(adam_kernel, float(count * n * rows * wi...  4.38 us

commit v1 on v0

v1 whole, which is shorter than its diff:
```python
import functools

import jax
import jax.numpy as jnp
from jax import lax
from jax.experimental import pallas as pl
from jax.experimental.pallas import tpu as pltpu
from jax.sharding import PartitionSpec as P

HEADS = 16
KV_HEADS = 8
HEAD_DIM = 128
GROUP = 128

score_scale = 144.0 ** (-0.5)
soft_cap = 50.0
beta_first = 0.9
beta_second = 0.95
learn_rate = 0.001
decay_rate = 0.1

MESH = pl.DeviceIdType.MESH


def longest(length):
    return length * 5 // 8


def reach_skips(tokens, n):
    skips = []
    for s in range(1, n):
        skip = max(0, s * tokens - longest(n * tokens)) // 128 * 128
        if skip < tokens:
            skips.append(skip)
    return tuple(skips)


def orders(bits):
    high = list(range(1, bits))
    return (high, high[::-1])


def flip(me, r):
    out = me
    b = 0
    while (1 << b) <= r:
        if r & (1 << b):
            digit = lax.rem(lax.div(me, 1 << b), 2)
            out = out + (1 - 2 * digit) * (1 << b)
        b += 1
    return out


def greet_bits(me, z, bits, n):
    barrier = pltpu.get_barrier_semaphore()
    for b in range(bits):
        pl.semaphore_signal(
            barrier, inc=1, device_id={"dp": flip(me, 1 << b), "seq": z}, device_id_type=MESH
        )
    for s in range(1, n):
        pl.semaphore_signal(
            barrier, inc=1, device_id={"dp": me, "seq": lax.rem(z + s, n)}, device_id_type=MESH
        )
    pl.semaphore_wait(barrier, bits + n - 1)


def main_kernel(
    bits, n, skips, ahead,
    q_ref, k_ref, v_ref, doc_ref, cot_ref, w_ref,
    out_ref, own_ref, sum_ref,
    kv_all, doc_all, w_all, att, own_doc, acc, tot,
    sb, rb, zs, zr, grad, tot_s, tot_r,
    ws, wr, ks, kr, ds_, dr, ts, tr, bs, br, zss, zsr, qs, qr,
):
    me = lax.axis_index("dp")
    z = lax.axis_index("seq")
    tokens = k_ref.shape[0]
    rows, width = w_ref.shape
    half = width // 2
    big = n * rows
    count = 1 << bits
    per = count // KV_HEADS
    steps = len(skips)
    right, left = lax.rem(z + 1, n), lax.rem(z + n - 1, n)
    group_me = lax.div(me, per)
    sends = []

    def descriptor(src, dst, ssem, rsem, dp, seq):
        return pltpu.make_async_remote_copy(
            src_ref=src, dst_ref=dst, send_sem=ssem, recv_sem=rsem,
            device_id={"dp": dp, "seq": seq}, device_id_type=MESH,
        )

    def go(make, cond=None):
        if cond is None:
            make().start()
        else:

            @pl.when(cond)
            def _():
                make().start()

        sends.append((make, cond))

    def when(cond, act):
        if cond is None:
            act()
        else:
            pl.when(cond)(act)

    own_rows = pl.ds(pl.multiple_of(z * tokens, 128), tokens)

    def restore_group(g, _):
        cols = pl.ds(pl.multiple_of(g * HEAD_DIM, 128), HEAD_DIM)
        for part, ref in enumerate((k_ref, v_ref)):
            x = ref[:, cols].astype(jnp.float32)
            scale = jnp.max(jnp.abs(x), axis=-1, keepdims=True) + 1e-06
            wide = scale.astype(jnp.bfloat16).astype(jnp.float32)
            coded = (x / wide).astype(jnp.bfloat16).astype(jnp.float32)
            kv_all[g, part, own_rows, :] = (coded * wide).astype(jnp.bfloat16)
        return 0

    lax.fori_loop(0, KV_HEADS, restore_group, 0)
    doc_all[:, own_rows] = doc_ref[...]
    own_doc[...] = jnp.broadcast_to(doc_ref[0:1, :], (128, tokens)).T

    def w_rows(block, zz):
        return pl.ds(pl.multiple_of((block * n + zz) * rows, 16), rows)

    w_all[w_rows(me, z), :] = w_ref[...].astype(jnp.bfloat16)
    for s in range(1, steps + 1):
        if skips[s - 1]:

            @pl.when(z >= s)
            def _(s=s):
                stale = pl.ds(pl.multiple_of((z - s) * tokens, 128), skips[s - 1])
                for g in range(KV_HEADS):
                    for part in range(2):
                        kv_all[g, part, stale, :] = jnp.zeros(
                            (skips[s - 1], HEAD_DIM), jnp.bfloat16
                        )

    greet_bits(me, z, bits, n)

    def room(direction, s):
        if direction == 0:
            return (z >= s - 1) & (z < n - 1)
        return (z <= n - s) & (z > 0)

    def landed(direction, s):
        return z >= s if direction == 0 else z <= n - 1 - s

    def group_of(i):
        return flip(group_me, KV_HEADS - 1 - i)

    def kv_copy(s, i, at):
        skip = skips[s - 1]
        start = pl.multiple_of(at * tokens + skip, 128)
        part = kv_all.at[group_of(i), :, pl.ds(start, tokens - skip), :]
        return descriptor(part, part, ks.at[s - 1, i], kr.at[s - 1, i], me, right)

    def kv_send(s, i, cond):
        go(lambda: kv_copy(s, i, z - (s - 1)), cond)

    def kv_relay(i):
        for s in range(1, steps + 1):

            @pl.when(landed(0, s))
            def _(s=s):
                kv_copy(s, i, z - s).wait_recv()

            if s < steps:
                kv_send(s + 1, i, room(0, s + 1))

    def w_hop(direction, s, at):
        part = w_all.at[w_rows(me, at), :]
        return descriptor(
            part, part, ws.at[direction, s - 1], wr.at[direction, s - 1],
            me, right if direction == 0 else left,
        )

    def w_send(direction, s):
        at = z - (s - 1) if direction == 0 else z + (s - 1)
        go(lambda: w_hop(direction, s, at), room(direction, s))

    w_tree = [list(order) + [0] for order in orders(bits)]
    w_stage = []
    for h in range(2):
        seen, levels = [0], []
        for b in w_tree[h]:
            fresh = [r | (1 << b) for r in seen]
            levels.append(fresh)
            seen = seen + fresh
        w_stage.append(levels)

    def w_copy(zz, h, r, to):
        part = w_all.at[w_rows(flip(me, r), zz), pl.ds(h * half, half)]
        return part, to

    def w_forward(zz, h, r, cond):
        order = w_tree[h]
        last = -1
        for i, b in enumerate(order):
            if r & (1 << b):
                last = i
        for b in order[last + 1:]:
            nr = r | (1 << b)

            def make(b=b, nr=nr):
                part = w_all.at[w_rows(flip(me, r), zz), pl.ds(h * half, half)]
                return descriptor(
                    part, part, ts.at[zz, h, nr], tr.at[zz, h, nr], flip(me, 1 << b), z
                )

            go(make, cond)

    def w_wait(zz, h, r, cond):
        def act():
            part = w_all.at[w_rows(flip(me, r), zz), pl.ds(h * half, half)]
            descriptor(part, part, ts.at[zz, h, r], tr.at[zz, h, r], me, right).wait_recv()

        when(cond, act)

    def w_level(zz, level, cond):
        for j in range(len(w_stage[0][level])):
            for h in range(2):
                r = w_stage[h][level][j]
                w_wait(zz, h, r, cond)
                if level < bits - 1:
                    w_forward(zz, h, r, cond)

    def w_arrive(direction, s):
        zz = z - s if direction == 0 else z + s

        @pl.when(landed(direction, s))
        def _():
            w_hop(direction, s, zz).wait_recv()

        if s < n - 1:
            w_send(direction, s + 1)
        for h in range(2):
            w_forward(zz, h, 0, landed(direction, s))

    last_step = KV_HEADS
    events = {i: [] for i in range(last_step + 1)}

    def plan(i, act):
        events[min(i, last_step)].append(act)

    for level in range(bits - 1):
        plan(level, lambda level=level: w_level(z, level, None))
    for s in range(1, n):
        at = 2 * (s - 1) * 3 // (n - 1)
        for direction in range(2):
            zz = z - s if direction == 0 else z + s
            plan(at, lambda d=direction, s=s: w_arrive(d, s))
            for level in range(bits - 1):
                plan(
                    at + 1 + level,
                    lambda zz=zz, level=level, d=direction, s=s: w_level(
                        zz, level, landed(d, s)
                    ),
                )

    for direction in range(2):
        w_send(direction, 1)
    for h in range(2):
        w_forward(z, h, 0, None)
    doc_copies = []
    for s in range(1, n):
        def make(s=s):
            slot = doc_all.at[:, own_rows]
            return descriptor(
                slot, slot, ds_.at[s - 1], dr.at[s - 1], me, lax.rem(z + s, n)
            )

        go(make)
        doc_copies.append(make)
    for i in range(KV_HEADS):
        kv_send(1, i, (z < n - 1) if i < ahead else ((z == 0) if n > 1 else None))

    query_at = lax.broadcasted_iota(jnp.int32, (tokens, tokens), 0)
    key_at = lax.broadcasted_iota(jnp.int32, (tokens, tokens), 1)
    lo = jnp.maximum(z - steps, 0)
    pair = HEADS // KV_HEADS

    def attend_group(i):
        g = group_of(i)
        acc[...] = jnp.zeros_like(acc)
        tot[...] = jnp.zeros_like(tot)

        def block(j, _):
            at = pl.ds(pl.multiple_of(j * tokens, 128), tokens)
            same = own_doc[:, 0:1] == doc_all[0:1, at]
            allowed = same & (key_at + (j - z) * tokens <= query_at)
            key = kv_all[g, 0, at, :]
            value = kv_all[g, 1, at, :]
            for hd in range(pair):
                cols = pl.ds(pl.multiple_of((g * pair + hd) * HEAD_DIM, 128), HEAD_DIM)
                scores = lax.dot_general(
                    q_ref[:, cols], key, (((1,), (1,)), ((), ())),
                    preferred_element_type=jnp.float32,
                )
                capped = soft_cap * jnp.tanh(scores * (score_scale / soft_cap))
                weights = jnp.where(allowed, jnp.exp(capped), 0.0)
                tot[hd] = tot[hd] + jnp.sum(weights, axis=-1, keepdims=True)
                acc[hd] = acc[hd] + jnp.dot(
                    weights.astype(jnp.bfloat16), value, preferred_element_type=jnp.float32
                )
            return 0

        lax.fori_loop(lo, z + 1, block, 0)
        for hd in range(pair):
            cols = pl.ds(pl.multiple_of((g * pair + hd) * HEAD_DIM, 128), HEAD_DIM)
            att[:, cols] = (acc[hd] / tot[hd]).astype(att.dtype)

    tree = [[0] + list(order) for order in orders(bits)]

    def first_bit(r, h):
        for b in tree[h]:
            if r & (1 << b):
                return b

    def sources(r, h):
        out = []
        for b in tree[h]:
            if r & (1 << b):
                break
            out.append(r | (1 << b))
        return out

    def block_t(r):
        start = pl.multiple_of(flip(me, r) * big, 128)
        return att[:, pl.ds(start, big)].T

    def reduce_block(r, h, block):
        value = jnp.dot(
            block, cot_ref[:, h * half:(h + 1) * half], preferred_element_type=jnp.float32
        )
        for src in sources(r, h):
            descriptor(
                sb.at[h, src], rb.at[h, src], bs.at[h, src], br.at[h, src], me, right
            ).wait_recv()
            value = value + rb[h, src].astype(jnp.float32)
        if r == 0:
            grad[:, h * half:(h + 1) * half] = value
            return
        sb[h, r] = value.astype(jnp.bfloat16)
        b = first_bit(r, h)
        go(lambda: descriptor(
            sb.at[h, r], rb.at[h, r], bs.at[h, r], br.at[h, r], flip(me, 1 << b), z
        ))

    late = []
    for i in range(KV_HEADS):
        kv_relay(i)
        if i + ahead < KV_HEADS:
            kv_send_next = i + ahead
            go(
                lambda j=kv_send_next: kv_copy(1, j, z), (z > 0) & (z < n - 1)
            )
        for act in events[i]:
            act()
        if i == 0:
            for make in doc_copies:
                make().wait_recv()
        attend_group(i)
        for r in range((KV_HEADS - i) * per - 1, (KV_HEADS - 1 - i) * per - 1, -1):
            if r == 0:
                continue
            block = block_t(r)
            for h in range(2):
                if len(sources(r, h)) > 1:
                    late.append((r, h))
                else:
                    reduce_block(r, h, block)
        if i == KV_HEADS - 2:
            for r, h in late:
                reduce_block(r, h, block_t(r))
            late = []
    for r, h in late:
        reduce_block(r, h, block_t(r))

    for act in events[last_step]:
        act()
    every = [(z, None)]
    for s in range(1, n):
        for direction in range(2):
            zz = z - s if direction == 0 else z + s
            every.append((zz, landed(direction, s)))
    for zz, cond in every:
        w_level(zz, bits - 1, cond)

    def project(c, _):
        cols = pl.ds(pl.multiple_of(c * 256, 256), 256)
        out_ref[:, cols] = jnp.dot(
            att[...], w_all[:, cols], preferred_element_type=jnp.float32
        ).astype(out_ref.dtype)
        return 0

    lax.fori_loop(0, width // 256, project, 0)

    last_block = block_t(0)
    for h in range(2):
        reduce_block(0, h, last_block)

    def part(zz, h):
        start = pl.multiple_of(zz * rows, 16)
        return grad[pl.ds(start, rows), h * half:(h + 1) * half]

    ring = {}
    for s in range(n):
        for h in range(2):
            shift = (2 * n - 1 - s) if h == 0 else (1 + s)
            at = lax.rem(z + shift, n)
            value = part(at, h)
            if s:
                ring[h, s - 1]().wait_recv()
                value = value + zr[h, s - 1].astype(jnp.float32)
            if s < n - 1:
                zs[h, s] = value.astype(jnp.bfloat16)

                def make(h=h, s=s):
                    return descriptor(
                        zs.at[h, s], zr.at[h, s], zss.at[h, s], zsr.at[h, s],
                        me, right if h == 0 else left,
                    )

                go(make)
                ring[h, s] = make
            else:
                own_ref[:, h * half:(h + 1) * half] = value

    own = own_ref[...]
    total = jnp.broadcast_to(
        jnp.sum(jnp.sum(own * own, axis=1, keepdims=True), axis=0, keepdims=True), (8, 128)
    )
    for b in range(bits):
        tot_s[b] = total

        def make(b=b):
            return descriptor(
                tot_s.at[b], tot_r.at[b], qs.at[b], qr.at[b], flip(me, 1 << b), z
            )

        go(make)
        make().wait_recv()
        total = total + tot_r[b]
    tot_s[bits] = total
    last = []
    for s in range(1, n):
        def make(s=s):
            i = bits + s - 1
            return descriptor(
                tot_s.at[bits], tot_r.at[i], qs.at[i], qr.at[i], me, lax.rem(z + s, n)
            )

        go(make)
        last.append(make)
    for s in range(1, n):
        last[s - 1]().wait_recv()
        total = total + tot_r[bits + s - 1]
    sum_ref[...] = total
    for make, cond in sends:
        when(cond, lambda make=make: make().wait_send())


def main_step(q, k, v, docs, cot, w, bits, n):
    tokens = k.shape[0]
    rows, width = w.shape
    half = width // 2
    count = 1 << bits
    skips = reach_skips(tokens, n)
    steps = len(skips)
    sem = pltpu.SemaphoreType.DMA
    vm = pl.BlockSpec(memory_space=pltpu.VMEM)
    pair = HEADS // KV_HEADS
    bf16, f32 = jnp.bfloat16, jnp.float32
    return pl.pallas_call(
        functools.partial(main_kernel, bits, n, skips, 2),
        out_shape=(
            jax.ShapeDtypeStruct((tokens, width), bf16),
            jax.ShapeDtypeStruct((rows, width), f32),
            jax.ShapeDtypeStruct((8, 128), f32),
        ),
        in_specs=[vm] * 6,
        out_specs=(vm,) * 3,
        scratch_shapes=[
            pltpu.VMEM((KV_HEADS, 2, n * tokens, HEAD_DIM), bf16),
            pltpu.VMEM((8, n * tokens), jnp.int32),
            pltpu.VMEM((count * n * rows, width), bf16),
            pltpu.VMEM((tokens, HEADS * HEAD_DIM), bf16),
            pltpu.VMEM((tokens, 128), jnp.int32),
            pltpu.VMEM((pair, tokens, HEAD_DIM), f32),
            pltpu.VMEM((pair, tokens, 1), f32),
            pltpu.VMEM((2, count, n * rows, half), bf16),
            pltpu.VMEM((2, count, n * rows, half), bf16),
            pltpu.VMEM((2, n - 1, rows, half), bf16),
            pltpu.VMEM((2, n - 1, rows, half), bf16),
            pltpu.VMEM((n * rows, width), f32),
            pltpu.VMEM((bits + 1, 8, 128), f32),
            pltpu.VMEM((bits + n - 1, 8, 128), f32),
            sem((2, n - 1)), sem((2, n - 1)),
            sem((steps, KV_HEADS)), sem((steps, KV_HEADS)),
            sem((n - 1,)), sem((n - 1,)),
            sem((n, 2, count)), sem((n, 2, count)),
            sem((2, count)), sem((2, count)),
            sem((2, n - 1)), sem((2, n - 1)),
            sem((bits + n - 1,)), sem((bits + n - 1,)),
        ],
        compiler_params=pltpu.CompilerParams(
            collective_id=0, has_side_effects=True, vmem_limit_bytes=62 * 1024 * 1024
        ),
    )(q, k, v, docs, cot, w)


def adam_kernel(
    entries,
    grad_ref, sum_ref, w_ref, m1_ref, s1_ref, m2_ref, s2_ref,
    nw_ref, n1_ref, ns1_ref, n2_ref, ns2_ref,
):
    width = w_ref.shape[1]
    rms = jnp.sqrt(sum_ref[0:1, :] / entries + 1e-06)
    factor = jnp.minimum(1.0, 1.0 / rms)

    def decode(coded, scale):
        x = coded.astype(jnp.float32)
        root = scale * jnp.sqrt(jnp.abs(x))
        return jnp.where(x < 0, -root, root)

    def encode(x):
        scale = jnp.max(jnp.abs(x), axis=-1, keepdims=True) + 1e-06
        return (x * jnp.abs(x) / (scale * scale)).astype(jnp.bfloat16), scale

    for g in range(width // GROUP):
        cols = slice(g * GROUP, (g + 1) * GROUP)
        clipped = grad_ref[:, cols] * factor
        first = beta_first * decode(m1_ref[:, cols], s1_ref[:, g:g + 1]) + (
            1.0 - beta_first
        ) * clipped
        second = (
            beta_second * decode(m2_ref[:, cols], s2_ref[:, g:g + 1])
            + (1.0 - beta_second) * clipped * clipped
        )
        weight = w_ref[:, cols]
        nw_ref[:, cols] = weight - learn_rate * (
            first / (jnp.sqrt(second) + 1e-08) + decay_rate * weight
        )
        n1_ref[:, cols], ns1_ref[:, g:g + 1] = encode(first)
        n2_ref[:, cols], ns2_ref[:, g:g + 1] = encode(second)


def adam(grad, total, weight, m1, s1, m2, s2, entries):
    vm = pl.BlockSpec(memory_space=pltpu.VMEM)
    like = lambda a: jax.ShapeDtypeStruct(a.shape, a.dtype)
    return pl.pallas_call(
        functools.partial(adam_kernel, entries),
        out_shape=(like(weight), like(m1), like(s1), like(m2), like(s2)),
        in_specs=[vm] * 7,
        out_specs=(vm,) * 5,
    )(grad, total, weight, m1, s1, m2, s2)


def local(
    bits, n,
    queries, keys, values, segments, cotangent, weight,
    first_moment, first_scale, second_moment, second_scale,
):
    docs = segments[0]
    tokens = docs.shape[0]
    rows, width = weight.shape
    layer_out, grad, total = main_step(
        queries[0], keys[0], values[0],
        jnp.broadcast_to(docs[None, :], (8, tokens)),
        cotangent[0], weight, bits, n,
    )
    entries = float((1 << bits) * n * rows * width)
    updated = adam(
        grad, total, weight, first_moment, first_scale, second_moment, second_scale, entries
    )
    return (layer_out[None], *updated)


def solution(mesh):
    bits = mesh.shape["dp"].bit_length() - 1
    n = mesh.shape["seq"]
    shard = P(("dp", "seq"), None)
    tok = P("dp", "seq", None)
    return jax.shard_map(
        functools.partial(local, bits, n),
        mesh=mesh,
        in_specs=(tok, tok, tok, P("dp", "seq"), tok, shard, shard, shard, shard, shard),
        out_specs=(tok, shard, shard, shard, shard, shard),
        check_vma=False,
    )
```

time: 204 us -> 160 us (0.78)
  Pallas kernels: 182 us -> 151 us
  matrix products: 7.29 us -> 0 us
  other arithmetic: 4.38 us -> 0 us
    pallas_call x4 -> x2, Pallas kernels: 182 us -> 151 us  [the longest x1 147 us: main_step(): pl.pallas_call(functools.partial(main_kernel, bits, n, skips, 2), out_sha...]
    dot_general x1 -> x0, matrix products: 7.29 us -> none  [local(): layer_out = jnp.dot(attended, w_all, preferred_element_type=jnp.float32)]
    convert_element_type x4 -> x0, other arithmetic: 2.43 us -> none  [the longest x1 1.67 us: restore(): (coded.astype(jnp.float32) * wide).astype(jnp.bfloat16)]
    pallas_call x1 -> x0, local copies, waits for them, and re-layouts: 2.27 us -> none  [attend(): pl.pallas_call(attend_kernel, grid=(KV_HEADS,), out_shape=jax.ShapeDtypeS...]
    unnamed x20 -> x7, local copies, waits for them, and re-layouts: 4.69 us -> 6.69 us
where the time goes in v1:
time: 160 us
  Pallas kernels  151 us (94%)
  local copies, waits for them, and re-layouts  7.97 us (5%)
    pallas_call x1, Pallas kernels, main_step(): pl.pallas_call(functools.partial(main_kernel, bits, n, skips, 2), out_sha...  147 us
    unnamed x7, local copies, waits for them, and re-layouts  6.69 us
    pallas_call x1, Pallas kernels, adam(): pl.pallas_call(functools.partial(adam_kernel, entries), out_shape=(like(w...  4.48 us

profile of v1, /device:TPU:0, one launch (start us, length us, event | category | flops | bytes accessed | tf_op | source)
XLA Modules:
  0.0 160.1 jit_solution(5670788244713135663)
XLA Ops:
  0.6 1.3 broadcast_in_dim.11.doc_ref
  1.9 1.4 copy.16.s1_ref
  3.3 1.4 copy.17.s2_ref
  4.7 147.0 %shard_map.145 = (bf16[256,2304]{1,0:T(8,128)(2,1)}, f32[64,2304]{1,0:T(8,128)}, f32[8,128]{1,0:T(8,128)}) custom-call(bf16[256,2048]{1,0:T(8,128)(2,1)} %bitcast.8, bf16[256,1024]{1,0:T(8,128)(2,1)} %bitcast.9, bf16[256,1024]{1,0:T(8,128)(2,1)} %bitcast.10, s32[8,256]{1,0:T(8,128)} %broadcast_in_dim.11.doc_ref, bf16[256,2304]{1,0:T(8,128)(2,1)} %bitcast.7, ...), custom_call_target="tpu_custom_call" | custom-call | tf_op jit(solution)/shard_map/pallas_call | solution.py:479
  151.7 0.0 copy-start
  151.7 4.5 %shard_map.146 = (f32[64,2304]{1,0:T(8,128)}, bf16[64,2304]{1,0:T(8,128)(2,1)}, f32[64,18]{1,0:T(8,128)}, bf16[64,2304]{1,0:T(8,128)(2,1)}, f32[64,18]{1,0:T(8,128)}) custom-call(f32[64,2304]{1,0:T(8,128)} %get-tuple-element.15.grad_ref, f32[8,128]{1,0:T(8,128)} %get-tuple-element.16.sum_ref, f32[64,2304]{1,0:T(8,128)} %w_ref.3, bf16[64,2304]{1,0:T(8,128)(2,1)} %m1_ref.1, ...), custom_call_target="tpu_custom_call" | custom-call | tf_op jit(solution)/shard_map/pallas_call | solution.py:556
  156.2 1.4 copy.18
  157.6 1.4 copy.19
  159.1 0.0 copy-done
  159.1 1.0 copy.21
Async XLA Ops:
  151.7 7.4 %copy-start = (bf16[256,2304]{1,0:T(8,128)(2,1)S(1)}, bf16[256,2304]{1,0:T(8,128)(2,1)}, u32[]{:S(2)}) copy-start(bf16[256,2304]{1,0:T(8,128)(2,1)} %get-tuple-element.14) | copy-start | bytes 3538948

commit v2 on v1

--- a/solution.py
+++ b/solution.py
@@ -121,7 +121,7 @@
         return 0
 
     lax.fori_loop(0, KV_HEADS, restore_group, 0)
-    doc_all[:, own_rows] = doc_ref[...]
+    doc_all[:, own_rows] = jnp.broadcast_to(doc_ref[...], (8, tokens))
     own_doc[...] = jnp.broadcast_to(doc_ref[0:1, :], (128, tokens)).T
 
     def w_rows(block, zz):
@@ -193,10 +193,6 @@
             seen = seen + fresh
         w_stage.append(levels)
 
-    def w_copy(zz, h, r, to):
-        part = w_all.at[w_rows(flip(me, r), zz), pl.ds(h * half, half)]
-        return part, to
-
     def w_forward(zz, h, r, cond):
         order = w_tree[h]
         last = -1
@@ -229,43 +225,43 @@
                 if level < bits - 1:
                     w_forward(zz, h, r, cond)
 
+    def source(direction, s):
+        return z - s if direction == 0 else z + s
+
     def w_arrive(direction, s):
-        zz = z - s if direction == 0 else z + s
+        zz = source(direction, s)
 
         @pl.when(landed(direction, s))
         def _():
             w_hop(direction, s, zz).wait_recv()
 
-        if s < n - 1:
-            w_send(direction, s + 1)
         for h in range(2):
             w_forward(zz, h, 0, landed(direction, s))
 
+    def arrive(s):
+        for direction in range(2):
+            w_arrive(direction, s)
+
+    def level(s, k):
+        if s == 0:
+            w_level(z, k, None)
+        else:
+            for direction in range(2):
+                w_level(source(direction, s), k, landed(direction, s))
+
     last_step = KV_HEADS
-    events = {i: [] for i in range(last_step + 1)}
+    events = {i: [] for i in range(last_step)}
 
     def plan(i, act):
-        events[min(i, last_step)].append(act)
-
-    for level in range(bits - 1):
-        plan(level, lambda level=level: w_level(z, level, None))
-    for s in range(1, n):
-        at = 2 * (s - 1) * 3 // (n - 1)
-        for direction in range(2):
-            zz = z - s if direction == 0 else z + s
-            plan(at, lambda d=direction, s=s: w_arrive(d, s))
-            for level in range(bits - 1):
-                plan(
-                    at + 1 + level,
-                    lambda zz=zz, level=level, d=direction, s=s: w_level(
-                        zz, level, landed(d, s)
-                    ),
-                )
-
-    for direction in range(2):
-        w_send(direction, 1)
-    for h in range(2):
-        w_forward(z, h, 0, None)
+        events[min(i, last_step - 1)].append(act)
+
+    plan(3, lambda: w_send(0, 1))
+    for k in range(bits - 1):
+        plan(2 + 2 * k, lambda k=k: level(0, k))
+    if n > 1:
+        plan(6, lambda: arrive(1))
+
+    w_send(1, 1)
     doc_copies = []
     for s in range(1, n):
         def make(s=s):
@@ -277,7 +273,9 @@
         go(make)
         doc_copies.append(make)
     for i in range(KV_HEADS):
-        kv_send(1, i, (z < n - 1) if i < ahead else ((z == 0) if n > 1 else None))
+        kv_send(1, i, (z < n - 1) if i < ahead else (z == 0))
+    for h in range(2):
+        w_forward(z, h, 0, None)
 
     query_at = lax.broadcasted_iota(jnp.int32, (tokens, tokens), 0)
     key_at = lax.broadcasted_iota(jnp.int32, (tokens, tokens), 1)
@@ -365,51 +363,26 @@
             for make in doc_copies:
                 make().wait_recv()
         attend_group(i)
+        for r, h in late:
+            reduce_block(r, h, block_t(r))
+        late = []
         for r in range((KV_HEADS - i) * per - 1, (KV_HEADS - 1 - i) * per - 1, -1):
             if r == 0:
                 continue
             block = block_t(r)
             for h in range(2):
-                if len(sources(r, h)) > 1:
+                if len(sources(r, h)) > 1 and i < 4:
                     late.append((r, h))
                 else:
                     reduce_block(r, h, block)
-        if i == KV_HEADS - 2:
-            for r, h in late:
-                reduce_block(r, h, block_t(r))
-            late = []
-    for r, h in late:
-        reduce_block(r, h, block_t(r))
-
-    for act in events[last_step]:
-        act()
-    every = [(z, None)]
-    for s in range(1, n):
-        for direction in range(2):
-            zz = z - s if direction == 0 else z + s
-            every.append((zz, landed(direction, s)))
-    for zz, cond in every:
-        w_level(zz, bits - 1, cond)
-
-    def project(c, _):
-        cols = pl.ds(pl.multiple_of(c * 256, 256), 256)
-        out_ref[:, cols] = jnp.dot(
-            att[...], w_all[:, cols], preferred_element_type=jnp.float32
-        ).astype(out_ref.dtype)
-        return 0
-
-    lax.fori_loop(0, width // 256, project, 0)
-
-    last_block = block_t(0)
-    for h in range(2):
-        reduce_block(0, h, last_block)
 
     def part(zz, h):
         start = pl.multiple_of(zz * rows, 16)
         return grad[pl.ds(start, rows), h * half:(h + 1) * half]
 
     ring = {}
-    for s in range(n):
+
+    def ring_step(s):
         for h in range(2):
             shift = (2 * n - 1 - s) if h == 0 else (1 + s)
             at = lax.rem(z + shift, n)
@@ -430,6 +403,28 @@
                 ring[h, s] = make
             else:
                 own_ref[:, h * half:(h + 1) * half] = value
+
+    def relay_w(s):
+        for direction in range(2):
+            w_send(direction, s)
+
+    if n > 2:
+        relay_w(2)
+        arrive(2)
+    if n > 3:
+        relay_w(3)
+    last_block = block_t(0)
+    for h in range(2):
+        reduce_block(0, h, last_block)
+    for s in range(n):
+        ring_step(s)
+        if s + 3 < n:
+            arrive(s + 3)
+            if s + 4 < n:
+                relay_w(s + 4)
+        if 0 < s < n - 1:
+            for k in range(min(s, bits - 1)):
+                level(s - k, k)
 
     own = own_ref[...]
     total = jnp.broadcast_to(
@@ -461,6 +456,23 @@
         last[s - 1]().wait_recv()
         total = total + tot_r[bits + s - 1]
     sum_ref[...] = total
+
+    done = {s: max(0, min(bits - 1, n - 1 - s)) for s in range(1, n)}
+    for k in range(bits - 1):
+        for s in range(1, n):
+            if k >= done[s]:
+                level(s, k)
+    for s in range(n):
+        level(s, bits - 1)
+
+    def project(c, _):
+        cols = pl.ds(pl.multiple_of(c * 256, 256), 256)
+        out_ref[:, cols] = jnp.dot(
+            att[...], w_all[:, cols], preferred_element_type=jnp.float32
+        ).astype(out_ref.dtype)
+        return 0
+
+    lax.fori_loop(0, width // 256, project, 0)
     for make, cond in sends:
         when(cond, lambda make=make: make().wait_send())
 
@@ -509,7 +521,7 @@
             sem((bits + n - 1,)), sem((bits + n - 1,)),
         ],
         compiler_params=pltpu.CompilerParams(
-            collective_id=0, has_side_effects=True, vmem_limit_bytes=62 * 1024 * 1024
+            collective_id=0, has_side_effects=True, vmem_limit_bytes=54 * 1024 * 1024
         ),
     )(q, k, v, docs, cot, w)
 
@@ -518,10 +530,17 @@
     entries,
     grad_ref, sum_ref, w_ref, m1_ref, s1_ref, m2_ref, s2_ref,
     nw_ref, n1_ref, ns1_ref, n2_ref, ns2_ref,
+    wide1, wide2, tall1, tall2,
 ):
-    width = w_ref.shape[1]
+    rows, width = w_ref.shape
+    groups = width // GROUP
     rms = jnp.sqrt(sum_ref[0:1, :] / entries + 1e-06)
     factor = jnp.minimum(1.0, 1.0 / rms)
+    for wide, ref in ((wide1, s1_ref), (wide2, s2_ref)):
+        wide[...] = jnp.zeros_like(wide)
+        wide[0:groups, 0:rows] = ref[...]
+    tall1[...] = wide1[...].T
+    tall2[...] = wide2[...].T
 
     def decode(coded, scale):
         x = coded.astype(jnp.float32)
@@ -532,33 +551,43 @@
         scale = jnp.max(jnp.abs(x), axis=-1, keepdims=True) + 1e-06
         return (x * jnp.abs(x) / (scale * scale)).astype(jnp.bfloat16), scale
 
-    for g in range(width // GROUP):
+    for g in range(groups):
         cols = slice(g * GROUP, (g + 1) * GROUP)
         clipped = grad_ref[:, cols] * factor
-        first = beta_first * decode(m1_ref[:, cols], s1_ref[:, g:g + 1]) + (
+        first = beta_first * decode(m1_ref[:, cols], tall1[0:rows, g:g + 1]) + (
             1.0 - beta_first
         ) * clipped
         second = (
-            beta_second * decode(m2_ref[:, cols], s2_ref[:, g:g + 1])
+            beta_second * decode(m2_ref[:, cols], tall2[0:rows, g:g + 1])
             + (1.0 - beta_second) * clipped * clipped
         )
         weight = w_ref[:, cols]
         nw_ref[:, cols] = weight - learn_rate * (
             first / (jnp.sqrt(second) + 1e-08) + decay_rate * weight
         )
-        n1_ref[:, cols], ns1_ref[:, g:g + 1] = encode(first)
-        n2_ref[:, cols], ns2_ref[:, g:g + 1] = encode(second)
+        n1_ref[:, cols], tall1[0:rows, g:g + 1] = encode(first)
+        n2_ref[:, cols], tall2[0:rows, g:g + 1] = encode(second)
+    ns1_ref[...] = tall1[...].T[0:groups, 0:rows]
+    ns2_ref[...] = tall2[...].T[0:groups, 0:rows]
 
 
 def adam(grad, total, weight, m1, s1, m2, s2, entries):
+    rows, width = weight.shape
     vm = pl.BlockSpec(memory_space=pltpu.VMEM)
     like = lambda a: jax.ShapeDtypeStruct(a.shape, a.dtype)
-    return pl.pallas_call(
+    s1, s2 = s1.T, s2.T
+    lanes = pl.cdiv(rows, 128) * 128
+    deep = pl.cdiv(width // GROUP, 128) * 128
+    scratch = [pltpu.VMEM((deep, lanes), jnp.float32)] * 2
+    scratch += [pltpu.VMEM((lanes, deep), jnp.float32)] * 2
+    nw, n1, ns1, n2, ns2 = pl.pallas_call(
         functools.partial(adam_kernel, entries),
         out_shape=(like(weight), like(m1), like(s1), like(m2), like(s2)),
         in_specs=[vm] * 7,
         out_specs=(vm,) * 5,
+        scratch_shapes=scratch,
     )(grad, total, weight, m1, s1, m2, s2)
+    return nw, n1, ns1.T, n2, ns2.T
 
 
 def local(
@@ -566,13 +595,10 @@
     queries, keys, values, segments, cotangent, weight,
     first_moment, first_scale, second_moment, second_scale,
 ):
-    docs = segments[0]
-    tokens = docs.shape[0]
     rows, width = weight.shape
     layer_out, grad, total = main_step(
         queries[0], keys[0], values[0],
-        jnp.broadcast_to(docs[None, :], (8, tokens)),
-        cotangent[0], weight, bits, n,
+        segments, cotangent[0], weight, bits, n,
     )
     entries = float((1 << bits) * n * rows * width)
     updated = adam(

time: 160 us -> 145 us (0.906)
  Pallas kernels: 151 us -> 143 us
  local copies, waits for them, and re-layouts: 7.97 us -> 1.02 us
    pallas_call x1, Pallas kernels: 147 us -> 137 us  [main_step(): pl.pallas_call(functools.partial(main_kernel, bits, n, skips, 2), out_sha...]
    unnamed x7 -> x3, local copies, waits for them, and re-layouts: 6.69 us -> 1.02 us
where the time goes in v2:
time: 145 us; the launch traced here: 144 us
  Pallas kernels  143 us (99%)
    pallas_call x1, Pallas kernels, main_step(): pl.pallas_call(functools.partial(main_kernel, bits, n, skips, 2), out_sha...  137 us
    pallas_call x1, Pallas kernels, adam(): pl.pallas_call(functools.partial(adam_kernel, entries), out_shape=(like(w...  5.81 us

profile of v2, /device:TPU:0, one launch (start us, length us, event | category | flops | bytes accessed | tf_op | source)
XLA Modules:
  0.0 144.3 jit_solution(14161217739375045729)
XLA Ops:
  0.6 136.8 %shard_map.145 = (bf16[256,2304]{1,0:T(8,128)(2,1)}, f32[64,2304]{1,0:T(8,128)}, f32[8,128]{1,0:T(8,128)}) custom-call(bf16[256,2048]{1,0:T(8,128)(2,1)} %bitcast.11, bf16[256,1024]{1,0:T(8,128)(2,1)} %bitcast.12, bf16[256,1024]{1,0:T(8,128)(2,1)} %bitcast.13, s32[1,256]{1,0:T(1,128)} %doc_ref.1, bf16[256,2304]{1,0:T(8,128)(2,1)} %bitcast.10, f32[64,2304]{1,0:T(8,128)} %w_ref.3), custom_call_target="tpu_custom_call" | custom-call | tf_op jit(solution)/shard_map/pallas_call | solution.py:491
  137.4 0.0 copy-start
  137.4 5.8 %shard_map.146 = (f32[64,2304]{1,0:T(8,128)}, bf16[64,2304]{1,0:T(8,128)(2,1)}, f32[18,64]{1,0:T(8,128)}, bf16[64,2304]{1,0:T(8,128)(2,1)}, f32[18,64]{1,0:T(8,128)}) custom-call(f32[64,2304]{1,0:T(8,128)} %get-tuple-element.15.grad_ref, f32[8,128]{1,0:T(8,128)} %get-tuple-element.16.sum_ref, f32[64,2304]{1,0:T(8,128)} %w_ref.3, bf16[64,2304]{1,0:T(8,128)(2,1)} %m1_ref.1, ...), custom_call_target="tpu_custom_call" | custom-call | tf_op jit(solution)/shard_map/pallas_call | solution.py:583
  143.2 0.0 copy-done
  143.2 1.0 copy.17
Async XLA Ops:
  137.4 5.8 %copy-start = (bf16[256,2304]{1,0:T(8,128)(2,1)S(1)}, bf16[256,2304]{1,0:T(8,128)(2,1)}, u32[]{:S(2)}) copy-start(bf16[256,2304]{1,0:T(8,128)(2,1)} %get-tuple-element.14) | copy-start | bytes 3538948

commit v3 on v2

v3 whole, which is shorter than its diff:
```python
import functools

import jax
import jax.numpy as jnp
from jax import lax
from jax.experimental import pallas as pl
from jax.experimental.pallas import tpu as pltpu
from jax.sharding import PartitionSpec as P

HEADS = 16
KV_HEADS = 8
HEAD_DIM = 128
GROUP = 128

score_scale = 144.0 ** (-0.5)
soft_cap = 50.0
beta_first = 0.9
beta_second = 0.95
learn_rate = 0.001
decay_rate = 0.1

MESH = pl.DeviceIdType.MESH


def longest(length):
    return length * 5 // 8


def reach_skips(tokens, n):
    skips = []
    for s in range(1, n):
        skip = max(0, s * tokens - longest(n * tokens)) // 128 * 128
        if skip < tokens:
            skips.append(skip)
    return tuple(skips)


def orders(bits):
    high = list(range(1, bits))
    return (high, high[::-1])


def flip(me, r):
    out = me
    b = 0
    while (1 << b) <= r:
        if r & (1 << b):
            digit = lax.rem(lax.div(me, 1 << b), 2)
            out = out + (1 - 2 * digit) * (1 << b)
        b += 1
    return out


def greet(me, z, bits, n):
    barrier = pltpu.get_barrier_semaphore()
    for r in range(1, 1 << bits):
        pl.semaphore_signal(
            barrier, inc=1, device_id={"dp": flip(me, r), "seq": z}, device_id_type=MESH
        )
    for s in range(1, n):
        pl.semaphore_signal(
            barrier, inc=1, device_id={"dp": me, "seq": lax.rem(z + s, n)}, device_id_type=MESH
        )
    pl.semaphore_wait(barrier, (1 << bits) + n - 2)


def main_kernel(
    bits, n, skips, ahead,
    q_hbm, k_ref, v_ref, doc_ref, cot_hbm, w_ref,
    out_hbm, own_hbm, sum_ref,
    q_ref, cot_ref, out_ref, own_ref, io_sem, kv_all, doc_all, w_all, att, own_doc, top_doc, acc, tot, q_top, o_top, t_top,
    sb, rb, zs, zr, grad, tot_s, tot_r,
    ws, wr, ks, kr, ds_, dr, ts, tr, bs, br, zss, zsr, qs, qr, hs, hr,
):
    me = lax.axis_index("dp")
    z = lax.axis_index("seq")
    tokens = k_ref.shape[0]
    rows, width = w_ref.shape
    half = width // 2
    big = n * rows
    count = 1 << bits
    per = count // KV_HEADS
    steps = len(skips)
    right, left = lax.rem(z + 1, n), lax.rem(z + n - 1, n)
    group_me = lax.div(me, per)
    sends = []
    load_q = pltpu.make_async_copy(q_hbm, q_ref, io_sem.at[0])
    load_cot = pltpu.make_async_copy(cot_hbm, cot_ref, io_sem.at[1])
    load_q.start()
    load_cot.start()

    def descriptor(src, dst, ssem, rsem, dp, seq):
        return pltpu.make_async_remote_copy(
            src_ref=src, dst_ref=dst, send_sem=ssem, recv_sem=rsem,
            device_id={"dp": dp, "seq": seq}, device_id_type=MESH,
        )

    def go(make, cond=None):
        if cond is None:
            make().start()
        else:

            @pl.when(cond)
            def _():
                make().start()

        sends.append((make, cond))

    def flush(upto):
        now, sends[:] = sends[:upto], sends[upto:]
        while now:
            cond = now[0][1]
            same = 1
            while same < len(now) and now[same][1] is cond:
                same += 1
            batch, now = now[:same], now[same:]

            def act(batch=batch):
                for make, _ in batch:
                    make().wait_send()

            when(cond, act)

    def when(cond, act):
        if cond is None:
            act()
        else:
            pl.when(cond)(act)

    own_rows = pl.ds(pl.multiple_of(z * tokens, 128), tokens)

    def restore_group(g, _):
        cols = pl.ds(pl.multiple_of(g * HEAD_DIM, 128), HEAD_DIM)
        for part, ref in enumerate((k_ref, v_ref)):
            x = ref[:, cols].astype(jnp.float32)
            scale = jnp.max(jnp.abs(x), axis=-1, keepdims=True) + 1e-06
            wide = scale.astype(jnp.bfloat16).astype(jnp.float32)
            coded = (x / wide).astype(jnp.bfloat16).astype(jnp.float32)
            kv_all[g, part, own_rows, :] = (coded * wide).astype(jnp.bfloat16)
        return 0

    lax.fori_loop(0, KV_HEADS, restore_group, 0)
    doc_all[:, own_rows] = jnp.broadcast_to(doc_ref[...], (8, tokens))
    own_doc[...] = jnp.broadcast_to(doc_ref[0:1, :], (128, tokens)).T

    def w_rows(block, zz):
        return pl.ds(pl.multiple_of((block * n + zz) * rows, 16), rows)

    w_all[w_rows(me, z), :] = w_ref[...].astype(jnp.bfloat16)
    for s in range(1, min(steps, n - 2) + 1):
        if skips[s - 1]:

            @pl.when((z >= s) & (z < n - 1))
            def _(s=s):
                stale = pl.ds(pl.multiple_of((z - s) * tokens, 128), skips[s - 1])
                for g in range(KV_HEADS):
                    for part in range(2):
                        kv_all[g, part, stale, :] = jnp.zeros(
                            (skips[s - 1], HEAD_DIM), jnp.bfloat16
                        )

    greet(me, z, bits, n)

    def room(direction, s):
        if direction == 0:
            return (z >= s - 1) & (z < n - 1)
        return (z <= n - s) & (z > 0)

    def landed(direction, s):
        return z >= s if direction == 0 else z <= n - 1 - s

    def group_of(i):
        return flip(group_me, KV_HEADS - 1 - i)

    hops = min(steps, n - 2)
    top = n - 1

    def kv_room(s):
        return (z >= s - 1) & (z < top - 1)

    def kv_landed(s):
        return (z >= s) & (z < top)

    def kv_copy(s, i, at):
        skip = skips[s - 1]
        start = pl.multiple_of(at * tokens + skip, 128)
        part = kv_all.at[group_of(i), :, pl.ds(start, tokens - skip), :]
        return descriptor(part, part, ks.at[s - 1, i], kr.at[s - 1, i], me, right)

    def kv_send(s, i, cond):
        go(lambda: kv_copy(s, i, z - (s - 1)), cond)

    def kv_relay(i):
        for s in range(1, hops + 1):

            @pl.when(kv_landed(s))
            def _(s=s):
                kv_copy(s, i, z - s).wait_recv()

            if s < hops:
                kv_send(s + 1, i, kv_room(s + 1))

    def w_hop(direction, s, at):
        part = w_all.at[w_rows(me, at), :]
        return descriptor(
            part, part, ws.at[direction, s - 1], wr.at[direction, s - 1],
            me, right if direction == 0 else left,
        )

    def w_send(direction, s, cond=None):
        at = z - (s - 1) if direction == 0 else z + (s - 1)
        cond = room(direction, s) if cond is None else cond
        go(lambda: w_hop(direction, s, at), cond)

    w_tree = [list(order) + [0] for order in orders(bits)]
    w_stage = []
    for h in range(2):
        seen, levels = [0], []
        for b in w_tree[h]:
            fresh = [r | (1 << b) for r in seen]
            levels.append(fresh)
            seen = seen + fresh
        w_stage.append(levels)

    def w_forward(zz, h, r, cond):
        order = w_tree[h]
        last = -1
        for i, b in enumerate(order):
            if r & (1 << b):
                last = i
        for b in order[last + 1:]:
            nr = r | (1 << b)

            def make(b=b, nr=nr):
                part = w_all.at[w_rows(flip(me, r), zz), pl.ds(h * half, half)]
                return descriptor(
                    part, part, ts.at[zz, h, nr], tr.at[zz, h, nr], flip(me, 1 << b), z
                )

            go(make, cond)

    def w_wait(zz, h, r, cond):
        def act():
            part = w_all.at[w_rows(flip(me, r), zz), pl.ds(h * half, half)]
            descriptor(part, part, ts.at[zz, h, r], tr.at[zz, h, r], me, right).wait_recv()

        when(cond, act)

    def w_level(zz, level, cond):
        for j in range(len(w_stage[0][level])):
            for h in range(2):
                r = w_stage[h][level][j]
                w_wait(zz, h, r, cond)
                if level < bits - 1:
                    w_forward(zz, h, r, cond)

    def source(direction, s):
        return z - s if direction == 0 else z + s

    def source(direction, s):
        return z - s if direction == 0 else z + s

    def land(direction, s, cond):
        @pl.when(cond)
        def _():
            w_hop(direction, s, source(direction, s)).wait_recv()

    def spread(direction, s, cond):
        for h in range(2):
            w_forward(source(direction, s), h, 0, cond)

    def level(direction, s, k, cond=None):
        if s == 0:
            w_level(z, k, None)
        else:
            cond = landed(direction, s) if cond is None else cond
            w_level(source(direction, s), k, cond)

    events = {i: [] for i in range(KV_HEADS)}

    def plan(i, act):
        events[min(i, KV_HEADS - 1)].append(act)

    chunks = []

    def chunk(direction, s, cond, lands=None, spreads=None, sees=()):
        item = {"at": (direction, s, cond), "done": 0, "landed": False, "here": False}
        chunks.append(item)

        def touch():
            land(direction, s, cond)
            item["landed"] = True

        def come():
            if not item["landed"]:
                touch()
            spread(direction, s, cond)
            item["here"] = True

        def deeper():
            level(direction, s, item["done"], cond)
            item["done"] += 1

        item["come"], item["deeper"] = come, deeper
        if lands is not None:
            plan(lands, touch)
        if spreads is not None:
            plan(spreads, come)
        for i in sees[:bits - 1]:
            plan(i, deeper)

    def turn():
        for item in chunks:
            if item["here"] and item["done"] < bits - 1:
                item["deeper"]()

    at_top, helper, below = z == top, z == top - 1, (z > 0) & (z < top - 1)
    for k in range(bits - 1):
        plan(2 * k, lambda k=k: level(0, 0, k))
    chunk(1, 1, landed(1, 1), 1, 2, (7,))
    chunk(0, 1, at_top, None, 0, (1, 3))
    chunk(0, 1, helper & (z > 0), 0, 2, (7,))
    chunk(0, 1, below, None, 7)
    if n > 2:
        plan(1, lambda: w_send(1, 2))
        plan(0, lambda: w_send(0, 2, helper & (z > 0)))
        plan(7, lambda: w_send(0, 2, below))
        chunk(0, 2, at_top, None, 1, (4, 7))
        chunk(1, 2, landed(1, 2), 7, 7)
        chunk(0, 2, landed(0, 2) & (z < top))
    if n > 3:
        plan(7, lambda: w_send(1, 3))
    for s in range(3, n):
        chunk(0, s, landed(0, s))
        chunk(1, s, landed(1, s))

    pair = HEADS // KV_HEADS
    span = pair * HEAD_DIM

    def q_cols(i):
        return pl.ds(pl.multiple_of(group_of(i) * span, 128), span)

    def q_copy(i):
        return descriptor(
            q_ref.at[:, q_cols(i)], q_top.at[i], hs.at[0, i], hr.at[0, i], me, left
        )

    def o_copy(i):
        return descriptor(
            o_top.at[i], o_top.at[i], hs.at[1, i], hr.at[1, i], me, right
        )

    def t_copy(i):
        return descriptor(
            t_top.at[i], t_top.at[i], hs.at[2, i], hr.at[2, i], me, right
        )

    load_q.wait()
    doc_copies = []
    for s in range(1, n):
        def make(s=s):
            slot = doc_all.at[:, own_rows]
            return descriptor(
                slot, slot, ds_.at[s - 1], dr.at[s - 1], me, lax.rem(z + s, n)
            )

        go(make)
        doc_copies.append(make)
    for i in range(KV_HEADS):
        if hops:
            kv_send(1, i, kv_room(1) if i < ahead else (z == 0) & kv_room(1))
        go(lambda i=i: q_copy(i), z == top)
        if i == 0:
            w_send(0, 1, (z > 0) & (z < top))
        if i == 1:
            w_send(1, 1)
            w_send(0, 1, (z == 0) & (z < top))
    for h in range(2):
        w_forward(z, h, 0, None)

    query_at = lax.broadcasted_iota(jnp.int32, (tokens, tokens), 0)
    key_at = lax.broadcasted_iota(jnp.int32, (tokens, tokens), 1)
    lo = jnp.where(z == top, z, jnp.maximum(z - steps, 0))

    def blocks(g, query, docs_ref, at_block, first, stop):
        acc[...] = jnp.zeros_like(acc)
        tot[...] = jnp.zeros_like(tot)

        def block(j, _):
            at = pl.ds(pl.multiple_of(j * tokens, 128), tokens)
            same = docs_ref[:, 0:1] == doc_all[0:1, at]
            allowed = same & (key_at + (j - at_block) * tokens <= query_at)
            key = kv_all[g, 0, at, :]
            value = kv_all[g, 1, at, :]
            for hd in range(pair):
                scores = lax.dot_general(
                    query(hd), key, (((1,), (1,)), ((), ())),
                    preferred_element_type=jnp.float32,
                )
                capped = soft_cap * jnp.tanh(scores * (score_scale / soft_cap))
                weights = jnp.where(allowed, jnp.exp(capped), 0.0)
                tot[hd] = tot[hd] + jnp.sum(weights, axis=-1, keepdims=True)
                acc[hd] = acc[hd] + jnp.dot(
                    weights.astype(jnp.bfloat16), value, preferred_element_type=jnp.float32
                )
            return 0

        lax.fori_loop(first, stop, block, 0)

    def attend_for_top(i):
        g = group_of(i)
        q_copy(i).wait_recv()
        blocks(
            g, lambda hd: q_top[i, :, hd * HEAD_DIM:(hd + 1) * HEAD_DIM],
            top_doc, top, max(top - steps, 0), top,
        )
        for hd in range(pair):
            o_top[i, :, hd * HEAD_DIM:(hd + 1) * HEAD_DIM] = acc[hd].astype(jnp.bfloat16)
            line = jnp.broadcast_to(tot[hd], (tokens, 128)).T
            t_top[i, hd * 4:(hd + 1) * 4, :] = line[0:4, :]
        o_copy(i).start()
        t_copy(i).start()

    def attend_group(i):
        g = group_of(i)

        def query(hd):
            return q_ref[:, pl.ds(pl.multiple_of((g * pair + hd) * HEAD_DIM, 128), HEAD_DIM)]

        blocks(g, query, own_doc, z, lo, z + 1)

        @pl.when(z == top)
        def _():
            o_copy(i).wait_recv()
            t_copy(i).wait_recv()
            for hd in range(pair):
                part = o_top[i, :, hd * HEAD_DIM:(hd + 1) * HEAD_DIM]
                acc[hd] = acc[hd] + part.astype(jnp.float32)
                line = t_top[i, hd * 4:hd * 4 + 1, :]
                tot[hd] = tot[hd] + jnp.broadcast_to(line, (128, tokens)).T[:, 0:1]

        for hd in range(pair):
            cols = pl.ds(pl.multiple_of((g * pair + hd) * HEAD_DIM, 128), HEAD_DIM)
            att[:, cols] = (acc[hd] / tot[hd]).astype(att.dtype)

    tree = [[0] + list(order) for order in orders(bits)]

    def first_bit(r, h):
        for b in tree[h]:
            if r & (1 << b):
                return b

    def sources(r, h):
        out = []
        for b in tree[h]:
            if r & (1 << b):
                break
            out.append(r | (1 << b))
        return out

    def block_t(r):
        start = pl.multiple_of(flip(me, r) * big, 128)
        return att[:, pl.ds(start, big)].T

    def reduce_block(r, h, block):
        value = jnp.dot(
            block, cot_ref[:, h * half:(h + 1) * half], preferred_element_type=jnp.float32
        )
        for src in sources(r, h):
            descriptor(
                sb.at[h, src], rb.at[h, src], bs.at[h, src], br.at[h, src], me, right
            ).wait_recv()
            value = value + rb[h, src].astype(jnp.float32)
        if r == 0:
            grad[:, h * half:(h + 1) * half] = value
            return
        sb[h, r] = value.astype(jnp.bfloat16)
        b = first_bit(r, h)
        go(lambda: descriptor(
            sb.at[h, r], rb.at[h, r], bs.at[h, r], br.at[h, r], flip(me, 1 << b), z
        ))

    late = []
    for i in range(KV_HEADS):
        if i == KV_HEADS // 2:
            early = len(sends)
        kv_relay(i)
        if hops and i + ahead < KV_HEADS:
            kv_send_next = i + ahead
            go(
                lambda j=kv_send_next: kv_copy(1, j, z), (z > 0) & kv_room(1)
            )
        for act in events[i]:
            act()
        if i == 0:
            load_cot.wait()
            for make in doc_copies:
                make().wait_recv()
            line = doc_all[0:1, top * tokens:(top + 1) * tokens]
            top_doc[...] = jnp.broadcast_to(line, (128, tokens)).T

        @pl.when(z == top - 1)
        def _():
            attend_for_top(i)

        attend_group(i)
        for r, h in late:
            reduce_block(r, h, block_t(r))
        late = []
        for r in range((KV_HEADS - i) * per - 1, (KV_HEADS - 1 - i) * per - 1, -1):
            if r == 0:
                continue
            block = block_t(r)
            for h in range(2):
                if len(sources(r, h)) > 1 and i < 4:
                    late.append((r, h))
                else:
                    reduce_block(r, h, block)

    lanes = (half // 128 + 1) // 2 * 128

    def ring_step(h, s):
        for direction in range(2):
            cut = slice(0, lanes) if direction == 0 else slice(lanes, half)
            cols = slice(h * half + cut.start, h * half + cut.stop)
            wide = cut.stop - cut.start
            q = 2 * h + direction
            shift = (2 * n - 1 - s) if direction == 0 else (1 + s)
            at = lax.rem(z + shift, n)

            def make(s, q=q, wide=wide, direction=direction):
                return descriptor(
                    zs.at[q, s, :, 0:wide], zr.at[q, s, :, 0:wide],
                    zss.at[q, s], zsr.at[q, s], me, right if direction == 0 else left,
                )

            value = grad[pl.ds(pl.multiple_of(at * rows, 16), rows), cols]
            if s:
                make(s - 1).wait_recv()
                value = value + zr[q, s - 1, :, 0:wide].astype(jnp.float32)
            if s < n - 1:
                zs[q, s, :, 0:wide] = value.astype(jnp.bfloat16)
                go(lambda make=make: make(s))
            else:
                own_ref[:, cols] = value

    def tail_arrive(s):
        for item in chunks:
            if item["at"][1] == s and not item["here"]:
                item["come"]()
        if s + 1 < n:
            w_send(0, s + 1)
            if s >= 3:
                w_send(1, s + 1)

    if n > 2:
        tail_arrive(2)
    last_block = block_t(0)
    reduce_block(0, 0, last_block)
    ring_step(0, 0)
    middle = len(sends) - early
    flush(early)
    ring_step(0, 1)
    reduce_block(0, 1, last_block)
    ring_step(1, 0)
    if n > 3:
        tail_arrive(3)
    flush(middle)

    @pl.when(z == top - 1)
    def _():
        for i in range(KV_HEADS):
            o_copy(i).wait_send()
            t_copy(i).wait_send()

    for s in range(2, n + 1):
        if s < n:
            ring_step(0, s)
        turn()
        ring_step(1, s - 1)
        if s + 2 < n:
            tail_arrive(s + 2)

    own = own_ref[...]
    save_own = pltpu.make_async_copy(own_ref, own_hbm, io_sem.at[2])
    save_own.start()
    total = jnp.broadcast_to(
        jnp.sum(jnp.sum(own * own, axis=1, keepdims=True), axis=0, keepdims=True), (8, 128)
    )
    for k in range(bits - 1):
        turn()

    def project(c, _):
        cols = pl.ds(pl.multiple_of(c * 256, 256), 256)
        out_ref[:, cols] = jnp.dot(
            att[...], w_all[:, cols], preferred_element_type=jnp.float32
        ).astype(out_ref.dtype)
        return 0

    tiles = width // 256
    mid = tiles // 2 * 256

    def save(cut, i):
        return pltpu.make_async_copy(out_ref.at[:, cut], out_hbm.at[:, cut], io_sem.at[i])

    save_left, save_right = save(slice(0, mid), 3), save(slice(mid, width), 4)
    stage = [
        [(r, flip(me, r), z) for r in range(1, count)],
        [(count + s - 1, me, lax.rem(z + s, n)) for s in range(1, n)],
    ]
    for j, peers in enumerate(stage):
        tot_s[j] = total
        for i, dp, seq in peers:
            go(lambda i=i, dp=dp, seq=seq, j=j: descriptor(
                tot_s.at[j], tot_r.at[i], qs.at[i], qr.at[i], dp, seq
            ))
        if j == 0:
            level(0, 0, bits - 1)
            for s in range(1, n):
                for direction in range(2):
                    level(direction, s, bits - 1)
            lax.fori_loop(0, tiles // 2, project, 0)
            save_left.start()
        else:
            lax.fori_loop(tiles // 2, tiles, project, 0)
            save_right.start()
        for i, dp, seq in peers:
            descriptor(
                tot_s.at[j], tot_r.at[i], qs.at[i], qr.at[i], dp, seq
            ).wait_recv()
            total = total + tot_r[i]
    sum_ref[...] = total
    flush(len(sends))
    save_own.wait()
    save_left.wait()
    save_right.wait()


def main_step(q, k, v, docs, cot, w, bits, n):
    tokens = k.shape[0]
    rows, width = w.shape
    half = width // 2
    count = 1 << bits
    skips = reach_skips(tokens, n)
    steps = len(skips)
    lanes = (half // 128 + 1) // 2 * 128
    sem = pltpu.SemaphoreType.DMA
    vm = pl.BlockSpec(memory_space=pltpu.VMEM)
    hbm = pl.BlockSpec(memory_space=pl.ANY)
    pair = HEADS // KV_HEADS
    bf16, f32 = jnp.bfloat16, jnp.float32
    return pl.pallas_call(
        functools.partial(main_kernel, bits, n, skips, 2),
        out_shape=(
            jax.ShapeDtypeStruct((tokens, width), bf16),
            jax.ShapeDtypeStruct((rows, width), f32),
            jax.ShapeDtypeStruct((8, 128), f32),
        ),
        in_specs=[hbm, vm, vm, vm, hbm, vm],
        out_specs=(hbm, hbm, vm),
        scratch_shapes=[
            pltpu.VMEM(q.shape, q.dtype),
            pltpu.VMEM(cot.shape, cot.dtype),
            pltpu.VMEM((tokens, width), bf16),
            pltpu.VMEM((rows, width), f32),
            sem((5,)),
            pltpu.VMEM((KV_HEADS, 2, n * tokens, HEAD_DIM), bf16),
            pltpu.VMEM((8, n * tokens), jnp.int32),
            pltpu.VMEM((count * n * rows, width), bf16),
            pltpu.VMEM((tokens, HEADS * HEAD_DIM), bf16),
            pltpu.VMEM((tokens, 128), jnp.int32),
            pltpu.VMEM((tokens, 128), jnp.int32),
            pltpu.VMEM((pair, tokens, HEAD_DIM), f32),
            pltpu.VMEM((pair, tokens, 1), f32),
            pltpu.VMEM((KV_HEADS, tokens, pair * HEAD_DIM), bf16),
            pltpu.VMEM((KV_HEADS, tokens, pair * HEAD_DIM), bf16),
            pltpu.VMEM((KV_HEADS, 8, tokens), f32),
            pltpu.VMEM((2, count, n * rows, half), bf16),
            pltpu.VMEM((2, count, n * rows, half), bf16),
            pltpu.VMEM((4, n - 1, rows, lanes), bf16),
            pltpu.VMEM((4, n - 1, rows, lanes), bf16),
            pltpu.VMEM((n * rows, width), f32),
            pltpu.VMEM((2, 8, 128), f32),
            pltpu.VMEM((count + n - 1, 8, 128), f32),
            sem((2, n - 1)), sem((2, n - 1)),
            sem((steps, KV_HEADS)), sem((steps, KV_HEADS)),
            sem((n - 1,)), sem((n - 1,)),
            sem((n, 2, count)), sem((n, 2, count)),
            sem((2, count)), sem((2, count)),
            sem((4, n - 1)), sem((4, n - 1)),
            sem((count + n - 1,)), sem((count + n - 1,)),
            sem((3, KV_HEADS)), sem((3, KV_HEADS)),
        ],
        compiler_params=pltpu.CompilerParams(
            collective_id=0, has_side_effects=True, vmem_limit_bytes=54 * 1024 * 1024
        ),
    )(q, k, v, docs, cot, w)


def adam_kernel(
    entries, tile,
    grad_ref, sum_ref, w_ref, m1_ref, s1_ref, m2_ref, s2_ref, layer_ref,
    nw_ref, n1_ref, ns1_ref, n2_ref, ns2_ref, layer_out_ref,
    wide, tall1, tall2, out1, out2, hold, sem,
):
    step = pl.program_id(0)
    take = pltpu.make_async_copy(layer_ref, hold, sem.at[0])
    give = pltpu.make_async_copy(hold, layer_out_ref, sem.at[1])

    @pl.when(step == 0)
    def _():
        take.start()

    @pl.when(step == 1)
    def _():
        take.wait()
        give.start()

    rows = w_ref.shape[0]
    groups = s1_ref.shape[0]
    rms = jnp.sqrt(sum_ref[0:1, :] / entries + 1e-06)
    factor = jnp.minimum(1.0, 1.0 / rms)
    lane = lax.broadcasted_iota(jnp.int32, tall1.shape, 1)

    @pl.when(step == 0)
    def _():
        for tall, ref in ((tall1, s1_ref), (tall2, s2_ref)):
            wide[...] = jnp.zeros_like(wide)
            wide[0:groups, 0:rows] = ref[...]
            tall[...] = wide[...].T

    def decode(coded, tall, g):
        x = coded.astype(jnp.float32)
        scale = jnp.sum(jnp.where(lane == g, tall[...], 0.0), axis=-1, keepdims=True)[0:rows]
        root = scale * jnp.sqrt(jnp.abs(x))
        return jnp.where(x < 0, -root, root)

    def encode(x, out, g):
        scale = jnp.max(jnp.abs(x), axis=-1, keepdims=True) + 1e-06
        out[0:rows] = jnp.where(lane[0:rows] == g, scale, out[0:rows])
        return (x * jnp.abs(x) / (scale * scale)).astype(jnp.bfloat16)

    for j in range(tile // GROUP):
        g = step * (tile // GROUP) + j
        cols = slice(j * GROUP, (j + 1) * GROUP)
        clipped = grad_ref[:, cols] * factor
        first = beta_first * decode(m1_ref[:, cols], tall1, g) + (
            1.0 - beta_first
        ) * clipped
        second = (
            beta_second * decode(m2_ref[:, cols], tall2, g)
            + (1.0 - beta_second) * clipped * clipped
        )
        weight = w_ref[:, cols]
        nw_ref[:, cols] = weight - learn_rate * (
            first / (jnp.sqrt(second) + 1e-08) + decay_rate * weight
        )
        n1_ref[:, cols] = encode(first, out1, g)
        n2_ref[:, cols] = encode(second, out2, g)

    @pl.when(step == pl.num_programs(0) - 1)
    def _():
        ns1_ref[...] = out1[...].T[0:groups, 0:rows]
        ns2_ref[...] = out2[...].T[0:groups, 0:rows]
        give.wait()


def adam(layer, grad, total, weight, m1, s1, m2, s2, entries):
    rows, width = weight.shape
    like = lambda a: jax.ShapeDtypeStruct(a.shape, a.dtype)
    s1, s2 = s1.T, s2.T
    lanes = pl.cdiv(rows, 128) * 128
    deep = pl.cdiv(width // GROUP, 128) * 128
    parts = 3
    tile = width // parts
    cut = pl.BlockSpec((rows, tile), lambda i: (0, i))
    whole = lambda a: pl.BlockSpec(a.shape, lambda i: (0, 0))
    scratch = [pltpu.VMEM((deep, lanes), jnp.float32)]
    scratch += [pltpu.VMEM((lanes, deep), jnp.float32)] * 4
    scratch += [pltpu.VMEM(layer.shape, layer.dtype), pltpu.SemaphoreType.DMA((2,))]
    far = pl.BlockSpec(memory_space=pl.ANY)
    nw, n1, ns1, n2, ns2, layer = pl.pallas_call(
        functools.partial(adam_kernel, entries, tile),
        grid=(parts,),
        out_shape=(like(weight), like(m1), like(s1), like(m2), like(s2), like(layer)),
        in_specs=[cut, whole(total), cut, cut, whole(s1), cut, whole(s2), far],
        out_specs=(cut, cut, whole(s1), cut, whole(s2), far),
        scratch_shapes=scratch,
    )(grad, total, weight, m1, s1, m2, s2, layer)
    return layer, nw, n1, ns1.T, n2, ns2.T


def local(
    bits, n,
    queries, keys, values, segments, cotangent, weight,
    first_moment, first_scale, second_moment, second_scale,
):
    rows, width = weight.shape
    layer_out, grad, total = main_step(
        queries[0], keys[0], values[0],
        segments, cotangent[0], weight, bits, n,
    )
    entries = float((1 << bits) * n * rows * width)
    layer_out, *updated = adam(
        layer_out, grad, total, weight,
        first_moment, first_scale, second_moment, second_scale, entries,
    )
    return (layer_out[None], *updated)


def solution(mesh):
    bits = mesh.shape["dp"].bit_length() - 1
    n = mesh.shape["seq"]
    shard = P(("dp", "seq"), None)
    tok = P("dp", "seq", None)
    return jax.shard_map(
        functools.partial(local, bits, n),
        mesh=mesh,
        in_specs=(tok, tok, tok, P("dp", "seq"), tok, shard, shard, shard, shard, shard),
        out_specs=(tok, shard, shard, shard, shard, shard),
        check_vma=False,
    )
```

time: 145 us -> 127 us (0.88)
  Pallas kernels: 143 us -> 126 us
    pallas_call x1, Pallas kernels: 137 us -> 122 us  [main_step(): pl.pallas_call(functools.partial(main_kernel, bits, n, skips, 2), out_sha...]
where the time goes in v3:
time: 127 us
  Pallas kernels  126 us (99%)
    pallas_call x1, Pallas kernels, main_step(): pl.pallas_call(functools.partial(main_kernel, bits, n, skips, 2), out_sha...  122 us
    pallas_call x1, Pallas kernels, adam(): pl.pallas_call(functools.partial(adam_kernel, entries, tile), grid=(parts...  4.42 us

profile of v3, /device:TPU:0, one launch (start us, length us, event | category | flops | bytes accessed | tf_op | source)
XLA Modules:
  0.0 126.8 jit_solution(4759335816586083763)
XLA Ops:
  0.6 121.6 %shard_map.145 = (bf16[256,2304]{1,0:T(8,128)(2,1)}, f32[64,2304]{1,0:T(8,128)}, f32[8,128]{1,0:T(8,128)}) custom-call(bf16[256,2048]{1,0:T(8,128)(2,1)} %bitcast.10, bf16[256,1024]{1,0:T(8,128)(2,1)} %bitcast.11, bf16[256,1024]{1,0:T(8,128)(2,1)} %bitcast.12, s32[1,256]{1,0:T(1,128)} %doc_ref.1, bf16[256,2304]{1,0:T(8,128)(2,1)} %bitcast.9, f32[64,2304]{1,0:T(8,128)} %w_ref.3), custom_call_target="tpu_custom_call" | custom-call | tf_op jit(solution)/shard_map/pallas_call | solution.py:652
  122.3 4.4 %shard_map.146 = (f32[64,2304]{1,0:T(8,128)}, bf16[64,2304]{1,0:T(8,128)(2,1)}, f32[18,64]{1,0:T(8,128)}, bf16[64,2304]{1,0:T(8,128)(2,1)}, f32[18,64]{1,0:T(8,128)}, /*index=5*/bf16[256,2304]{1,0:T(8,128)(2,1)}) custom-call(f32[64,2304]{1,0:T(8,128)} %get-tuple-element.15.grad_ref, f32[8,128]{1,0:T(8,128)} %get-tuple-element.16.sum_ref, f32[64,2304]{1,0:T(8,128)} %w_ref.3, ...), custom_call_target="tpu_custom_call" | custom-call | tf_op jit(solution)/shard_map/pallas_call | solution.py:782

commit v4 on v3

--- a/solution.py
+++ b/solution.py
@@ -69,8 +69,8 @@
     q_hbm, k_ref, v_ref, doc_ref, cot_hbm, w_ref,
     out_hbm, own_hbm, sum_ref,
     q_ref, cot_ref, out_ref, own_ref, io_sem, kv_all, doc_all, w_all, att, own_doc, top_doc, acc, tot, q_top, o_top, t_top,
-    sb, rb, zs, zr, grad, tot_s, tot_r,
-    ws, wr, ks, kr, ds_, dr, ts, tr, bs, br, zss, zsr, qs, qr, hs, hr,
+    sb, rb, zs, zr, grad, extra, own_extra, x_s, x_r, tot_s, tot_r,
+    ws, wr, ks, kr, ds_, dr, ts, tr, bs, br, zss, zsr, qs, qr, hs, hr, xs,
 ):
     me = lax.axis_index("dp")
     z = lax.axis_index("seq")
@@ -95,7 +95,7 @@
             device_id={"dp": dp, "seq": seq}, device_id_type=MESH,
         )
 
-    def go(make, cond=None):
+    def go(make, cond=None, keep=True):
         if cond is None:
             make().start()
         else:
@@ -104,7 +104,11 @@
             def _():
                 make().start()
 
-        sends.append((make, cond))
+        if keep:
+            sends.append((make, cond))
+
+    def sent(ref, sem):
+        descriptor(ref, ref, sem, sem, me, right).wait_send()
 
     def flush(upto):
         now, sends[:] = sends[:upto], sends[upto:]
@@ -185,10 +189,10 @@
         skip = skips[s - 1]
         start = pl.multiple_of(at * tokens + skip, 128)
         part = kv_all.at[group_of(i), :, pl.ds(start, tokens - skip), :]
-        return descriptor(part, part, ks.at[s - 1, i], kr.at[s - 1, i], me, right)
+        return descriptor(part, part, ks.at[s - 1], kr.at[s - 1, i], me, right)
 
     def kv_send(s, i, cond):
-        go(lambda: kv_copy(s, i, z - (s - 1)), cond)
+        go(lambda: kv_copy(s, i, z - (s - 1)), cond, False)
 
     def kv_relay(i):
         for s in range(1, hops + 1):
@@ -222,6 +226,9 @@
             seen = seen + fresh
         w_stage.append(levels)
 
+    def w_sem(zz, h, r):
+        return ts.at[1] if r % 2 else tr.at[zz, h, r // 2]
+
     def w_forward(zz, h, r, cond):
         order = w_tree[h]
         last = -1
@@ -234,15 +241,15 @@
             def make(b=b, nr=nr):
                 part = w_all.at[w_rows(flip(me, r), zz), pl.ds(h * half, half)]
                 return descriptor(
-                    part, part, ts.at[zz, h, nr], tr.at[zz, h, nr], flip(me, 1 << b), z
+                    part, part, ts.at[0], w_sem(zz, h, nr), flip(me, 1 << b), z
                 )
 
-            go(make, cond)
+            go(make, cond, False)
 
     def w_wait(zz, h, r, cond):
         def act():
             part = w_all.at[w_rows(flip(me, r), zz), pl.ds(h * half, half)]
-            descriptor(part, part, ts.at[zz, h, r], tr.at[zz, h, r], me, right).wait_recv()
+            descriptor(part, part, ts.at[0], w_sem(zz, h, r), me, right).wait_recv()
 
         when(cond, act)
 
@@ -283,8 +290,8 @@
 
     chunks = []
 
-    def chunk(direction, s, cond, lands=None, spreads=None, sees=()):
-        item = {"at": (direction, s, cond), "done": 0, "landed": False, "here": False}
+    def chunk(direction, s, cond, lands=None, spreads=None, sees=(), soon=False):
+        item = {"at": (direction, s, cond), "done": 0, "landed": False, "here": False, "soon": soon}
         chunks.append(item)
 
         def touch():
@@ -309,8 +316,10 @@
         for i in sees[:bits - 1]:
             plan(i, deeper)
 
-    def turn():
+    def turn(soon=False):
         for item in chunks:
+            if soon and not item["soon"]:
+                continue
             if item["here"] and item["done"] < bits - 1:
                 item["deeper"]()
 
@@ -319,14 +328,14 @@
         plan(2 * k, lambda k=k: level(0, 0, k))
     chunk(1, 1, landed(1, 1), 1, 2, (7,))
     chunk(0, 1, at_top, None, 0, (1, 3))
-    chunk(0, 1, helper & (z > 0), 0, 2, (7,))
-    chunk(0, 1, below, None, 7)
+    chunk(0, 1, helper & (z > 0), 0, 5, ())
+    chunk(0, 1, below, None, 7, soon=True)
     if n > 2:
         plan(1, lambda: w_send(1, 2))
         plan(0, lambda: w_send(0, 2, helper & (z > 0)))
         plan(7, lambda: w_send(0, 2, below))
-        chunk(0, 2, at_top, None, 1, (4, 7))
-        chunk(1, 2, landed(1, 2), 7, 7)
+        chunk(0, 2, at_top, None, 1, (4,), soon=True)
+        chunk(1, 2, landed(1, 2), 7, 7, soon=True)
         chunk(0, 2, landed(0, 2) & (z < top))
     if n > 3:
         plan(7, lambda: w_send(1, 3))
@@ -342,17 +351,17 @@
 
     def q_copy(i):
         return descriptor(
-            q_ref.at[:, q_cols(i)], q_top.at[i], hs.at[0, i], hr.at[0, i], me, left
+            q_ref.at[:, q_cols(i)], q_top.at[i], hs.at[0], hr.at[0, i], me, left
         )
 
     def o_copy(i):
         return descriptor(
-            o_top.at[i], o_top.at[i], hs.at[1, i], hr.at[1, i], me, right
+            o_top.at[i], o_top.at[i], hs.at[1], hr.at[1, i], me, right
         )
 
     def t_copy(i):
         return descriptor(
-            t_top.at[i], t_top.at[i], hs.at[2, i], hr.at[2, i], me, right
+            t_top.at[i], t_top.at[i], hs.at[2], hr.at[2, i], me, right
         )
 
     load_q.wait()
@@ -361,15 +370,15 @@
         def make(s=s):
             slot = doc_all.at[:, own_rows]
             return descriptor(
-                slot, slot, ds_.at[s - 1], dr.at[s - 1], me, lax.rem(z + s, n)
+                slot, slot, ds_.at[0], dr.at[s - 1], me, lax.rem(z + s, n)
             )
 
-        go(make)
+        go(make, None, False)
         doc_copies.append(make)
     for i in range(KV_HEADS):
         if hops:
             kv_send(1, i, kv_room(1) if i < ahead else (z == 0) & kv_room(1))
-        go(lambda i=i: q_copy(i), z == top)
+        go(lambda i=i: q_copy(i), z == top, False)
         if i == 0:
             w_send(0, 1, (z > 0) & (z < top))
         if i == 1:
@@ -458,6 +467,8 @@
             out.append(r | (1 << b))
         return out
 
+    ahead_of = 2
+
     def block_t(r):
         start = pl.multiple_of(flip(me, r) * big, 128)
         return att[:, pl.ds(start, big)].T
@@ -467,18 +478,81 @@
             block, cot_ref[:, h * half:(h + 1) * half], preferred_element_type=jnp.float32
         )
         for src in sources(r, h):
+            if (r, h) == (0, 1) and src == ahead_of:
+                continue
             descriptor(
-                sb.at[h, src], rb.at[h, src], bs.at[h, src], br.at[h, src], me, right
+                sb.at[h, src], rb.at[h, src], bs.at[h], br.at[h, src], me, right
             ).wait_recv()
             value = value + rb[h, src].astype(jnp.float32)
         if r == 0:
             grad[:, h * half:(h + 1) * half] = value
             return
+        if (r, h) == (ahead_of, 1):
+            extra[...] = value
+            return
         sb[h, r] = value.astype(jnp.bfloat16)
         b = first_bit(r, h)
         go(lambda: descriptor(
-            sb.at[h, r], rb.at[h, r], bs.at[h, r], br.at[h, r], flip(me, 1 << b), z
-        ))
+            sb.at[h, r], rb.at[h, r], bs.at[h], br.at[h, r], flip(me, 1 << b), z
+        ), None, False)
+
+    def x_copy():
+        return descriptor(x_s, x_r, xs.at[0], xs.at[1], flip(me, ahead_of), z)
+
+    def line_copy(job, direction, k):
+        return descriptor(
+            zs.at[job, direction, k], zr.at[job, direction, k],
+            zss.at[job, direction, k], zsr.at[job, direction, k],
+            me, right if direction == 0 else left,
+        )
+
+    def rows_of(job, dest):
+        at = pl.ds(pl.multiple_of(dest * rows, 16), rows)
+        if job == 2:
+            return extra[at, :]
+        return grad[at, job * half:(job + 1) * half]
+
+    def line_hop(job, direction, k, cond, relay):
+        dest = n - 1 - k if direction == 0 else k
+
+        @pl.when(cond)
+        def _():
+            value = rows_of(job, dest)
+            if relay:
+                line_copy(job, direction, k).wait_recv()
+                value = value + zr[job, direction, k].astype(jnp.float32)
+            zs[job, direction, k] = value.astype(jnp.bfloat16)
+            line_copy(job, direction, k).start()
+
+        sends.append((lambda: line_copy(job, direction, k), cond))
+
+    def line_push(job):
+        for k in range(n - 1):
+            line_hop(job, 0, k, z == 0, False)
+            line_hop(job, 1, k, z == top, False)
+
+    def line_relay(job, direction, only=True):
+        for k in range(n - 2):
+            if direction == 0:
+                line_hop(job, 0, k, (z > 0) & (z < n - 1 - k) & only, True)
+            else:
+                line_hop(job, 1, k, (z < top) & (z > k) & only, True)
+
+    def line_final(job):
+        target, cols = own_ref, slice(job * half, (job + 1) * half)
+        if job == 2:
+            target, cols = own_extra, slice(0, half)
+        target[:, cols] = rows_of(job, z)
+        for direction, cond, k in ((0, z > 0, top - z), (1, z < top, z)):
+
+            @pl.when(cond)
+            def _(direction=direction, k=k):
+                line_copy(job, direction, k).wait_recv()
+                target[:, cols] = target[:, cols] + zr[job, direction, k].astype(jnp.float32)
+
+        if job == 2:
+            x_s[...] = own_extra[...].astype(jnp.bfloat16)
+            go(x_copy)
 
     late = []
     for i in range(KV_HEADS):
@@ -488,7 +562,7 @@
         if hops and i + ahead < KV_HEADS:
             kv_send_next = i + ahead
             go(
-                lambda j=kv_send_next: kv_copy(1, j, z), (z > 0) & kv_room(1)
+                lambda j=kv_send_next: kv_copy(1, j, z), (z > 0) & kv_room(1), False
             )
         for act in events[i]:
             act()
@@ -516,33 +590,8 @@
                     late.append((r, h))
                 else:
                     reduce_block(r, h, block)
-
-    lanes = (half // 128 + 1) // 2 * 128
-
-    def ring_step(h, s):
-        for direction in range(2):
-            cut = slice(0, lanes) if direction == 0 else slice(lanes, half)
-            cols = slice(h * half + cut.start, h * half + cut.stop)
-            wide = cut.stop - cut.start
-            q = 2 * h + direction
-            shift = (2 * n - 1 - s) if direction == 0 else (1 + s)
-            at = lax.rem(z + shift, n)
-
-            def make(s, q=q, wide=wide, direction=direction):
-                return descriptor(
-                    zs.at[q, s, :, 0:wide], zr.at[q, s, :, 0:wide],
-                    zss.at[q, s], zsr.at[q, s], me, right if direction == 0 else left,
-                )
-
-            value = grad[pl.ds(pl.multiple_of(at * rows, 16), rows), cols]
-            if s:
-                make(s - 1).wait_recv()
-                value = value + zr[q, s - 1, :, 0:wide].astype(jnp.float32)
-            if s < n - 1:
-                zs[q, s, :, 0:wide] = value.astype(jnp.bfloat16)
-                go(lambda make=make: make(s))
-            else:
-                own_ref[:, cols] = value
+                if (r, h) == (ahead_of, 1):
+                    line_push(2)
 
     def tail_arrive(s):
         for item in chunks:
@@ -556,30 +605,52 @@
     if n > 2:
         tail_arrive(2)
     last_block = block_t(0)
+    reduce_block(0, 1, last_block)
+    line_push(1)
+    line_relay(2, 0)
+    line_relay(1, 0)
+    line_relay(2, 1)
+    turn(True)
+    line_relay(1, 1, helper)
+    if n > 3:
+        tail_arrive(3)
     reduce_block(0, 0, last_block)
-    ring_step(0, 0)
+    line_push(0)
+    line_relay(0, 0)
+    line_relay(1, 1, z < top - 1)
+    line_final(2)
     middle = len(sends) - early
     flush(early)
-    ring_step(0, 1)
-    reduce_block(0, 1, last_block)
-    ring_step(1, 0)
-    if n > 3:
-        tail_arrive(3)
-    flush(middle)
+    line_final(1)
+    line_relay(0, 1)
+    for s in range(4, n):
+        turn()
+        tail_arrive(s)
+    turn()
+    turn()
+    line_final(0)
 
     @pl.when(z == top - 1)
     def _():
-        for i in range(KV_HEADS):
-            o_copy(i).wait_send()
-            t_copy(i).wait_send()
-
-    for s in range(2, n + 1):
-        if s < n:
-            ring_step(0, s)
-        turn()
-        ring_step(1, s - 1)
-        if s + 2 < n:
-            tail_arrive(s + 2)
+        sent(o_top, hs.at[1])
+        sent(t_top, hs.at[2])
+
+    @pl.when(z == top)
+    def _():
+        sent(q_top, hs.at[0])
+
+    for s in range(1, hops + 1):
+
+        @pl.when(kv_room(s))
+        def _(s=s):
+            sent(kv_all.at[:, :, 0:tokens - skips[s - 1], :], ks.at[s - 1])
+
+    sent(doc_all.at[:, 0:(n - 1) * tokens], ds_.at[0])
+    sent(sb.at[0, 1:count], bs.at[0])
+    sent(sb.at[1, 0:count - 2], bs.at[1])
+
+    x_copy().wait_recv()
+    own_ref[:, half:] = own_ref[:, half:] + x_r[...].astype(jnp.float32)
 
     own = own_ref[...]
     save_own = pltpu.make_async_copy(own_ref, own_hbm, io_sem.at[2])
@@ -612,24 +683,23 @@
         tot_s[j] = total
         for i, dp, seq in peers:
             go(lambda i=i, dp=dp, seq=seq, j=j: descriptor(
-                tot_s.at[j], tot_r.at[i], qs.at[i], qr.at[i], dp, seq
-            ))
+                tot_s.at[j], tot_r.at[i], qs.at[j], qr.at[j], dp, seq
+            ), None, False)
         if j == 0:
-            level(0, 0, bits - 1)
-            for s in range(1, n):
-                for direction in range(2):
-                    level(direction, s, bits - 1)
+            got = w_all.at[0:n * count // 2 * rows, :]
+            descriptor(got, got, ts.at[0], ts.at[1], me, right).wait_recv()
             lax.fori_loop(0, tiles // 2, project, 0)
             save_left.start()
         else:
             lax.fori_loop(tiles // 2, tiles, project, 0)
             save_right.start()
-        for i, dp, seq in peers:
-            descriptor(
-                tot_s.at[j], tot_r.at[i], qs.at[i], qr.at[i], dp, seq
-            ).wait_recv()
+        got = tot_r.at[peers[0][0]:peers[-1][0] + 1]
+        descriptor(got, got, qs.at[j], qr.at[j], me, right).wait_recv()
+        for i, _, _ in peers:
             total = total + tot_r[i]
+        sent(got, qs.at[j])
     sum_ref[...] = total
+    sent(w_all.at[0:n * (count - 1) * rows, :], ts.at[0])
     flush(len(sends))
     save_own.wait()
     save_left.wait()
@@ -642,8 +712,7 @@
     half = width // 2
     count = 1 << bits
     skips = reach_skips(tokens, n)
-    steps = len(skips)
-    lanes = (half // 128 + 1) // 2 * 128
+    hops = min(len(skips), n - 2)
     sem = pltpu.SemaphoreType.DMA
     vm = pl.BlockSpec(memory_space=pltpu.VMEM)
     hbm = pl.BlockSpec(memory_space=pl.ANY)
@@ -677,22 +746,27 @@
             pltpu.VMEM((KV_HEADS, 8, tokens), f32),
             pltpu.VMEM((2, count, n * rows, half), bf16),
             pltpu.VMEM((2, count, n * rows, half), bf16),
-            pltpu.VMEM((4, n - 1, rows, lanes), bf16),
-            pltpu.VMEM((4, n - 1, rows, lanes), bf16),
+            pltpu.VMEM((3, 2, n - 1, rows, half), bf16),
+            pltpu.VMEM((3, 2, n - 1, rows, half), bf16),
             pltpu.VMEM((n * rows, width), f32),
+            pltpu.VMEM((n * rows, half), f32),
+            pltpu.VMEM((rows, half), f32),
+            pltpu.VMEM((rows, half), bf16),
+            pltpu.VMEM((rows, half), bf16),
             pltpu.VMEM((2, 8, 128), f32),
             pltpu.VMEM((count + n - 1, 8, 128), f32),
             sem((2, n - 1)), sem((2, n - 1)),
-            sem((steps, KV_HEADS)), sem((steps, KV_HEADS)),
-            sem((n - 1,)), sem((n - 1,)),
-            sem((n, 2, count)), sem((n, 2, count)),
-            sem((2, count)), sem((2, count)),
-            sem((4, n - 1)), sem((4, n - 1)),
-            sem((count + n - 1,)), sem((count + n - 1,)),
-            sem((3, KV_HEADS)), sem((3, KV_HEADS)),
+            sem((max(hops, 1),)), sem((max(hops, 1), KV_HEADS)),
+            sem((1,)), sem((n - 1,)),
+            sem((2,)), sem((n, 2, count // 2)),
+            sem((2,)), sem((2, count)),
+            sem((3, 2, n - 1)), sem((3, 2, n - 1)),
+            sem((2,)), sem((2,)),
+            sem((3,)), sem((3, KV_HEADS)),
+            sem((2,)),
         ],
         compiler_params=pltpu.CompilerParams(
-            collective_id=0, has_side_effects=True, vmem_limit_bytes=54 * 1024 * 1024
+            collective_id=0, has_side_effects=True, vmem_limit_bytes=60 * 1024 * 1024
         ),
     )(q, k, v, docs, cot, w)
 

time: 127 us -> 117 us (0.921)
  Pallas kernels: 126 us -> 116 us
    pallas_call x1, Pallas kernels: 122 us -> 111 us  [main_step(): pl.pallas_call(functools.partial(main_kernel, bits, n, skips, 2), out_sha...]
where the time goes in v4:
time: 117 us; the launch traced here: 116 us
  Pallas kernels  116 us (99%)
    pallas_call x1, Pallas kernels, main_step(): pl.pallas_call(functools.partial(main_kernel, bits, n, skips, 2), out_sha...  111 us
    pallas_call x1, Pallas kernels, adam(): pl.pallas_call(functools.partial(adam_kernel, entries, tile), grid=(parts...  4.42 us

profile of v4, /device:TPU:0, one launch (start us, length us, event | category | flops | bytes accessed | tf_op | source)
XLA Modules:
  0.0 116.4 jit_solution(18224175131425560516)
XLA Ops:
  0.6 111.2 %shard_map.145 = (bf16[256,2304]{1,0:T(8,128)(2,1)}, f32[64,2304]{1,0:T(8,128)}, f32[8,128]{1,0:T(8,128)}) custom-call(bf16[256,2048]{1,0:T(8,128)(2,1)} %bitcast.10, bf16[256,1024]{1,0:T(8,128)(2,1)} %bitcast.11, bf16[256,1024]{1,0:T(8,128)(2,1)} %bitcast.12, s32[1,256]{1,0:T(1,128)} %doc_ref.1, bf16[256,2304]{1,0:T(8,128)(2,1)} %bitcast.9, f32[64,2304]{1,0:T(8,128)} %w_ref.3), custom_call_target="tpu_custom_call" | custom-call | tf_op jit(solution)/shard_map/pallas_call | solution.py:721
  111.9 4.4 %shard_map.146 = (f32[64,2304]{1,0:T(8,128)}, bf16[64,2304]{1,0:T(8,128)(2,1)}, f32[18,64]{1,0:T(8,128)}, bf16[64,2304]{1,0:T(8,128)(2,1)}, f32[18,64]{1,0:T(8,128)}, /*index=5*/bf16[256,2304]{1,0:T(8,128)(2,1)}) custom-call(f32[64,2304]{1,0:T(8,128)} %get-tuple-element.15.grad_ref, f32[8,128]{1,0:T(8,128)} %get-tuple-element.16.sum_ref, f32[64,2304]{1,0:T(8,128)} %w_ref.3, ...), custom_call_target="tpu_custom_call" | custom-call | tf_op jit(solution)/shard_map/pallas_call | solution.py:856

commit v5 on v4

--- a/solution.py
+++ b/solution.py
@@ -133,6 +133,9 @@
 
     own_rows = pl.ds(pl.multiple_of(z * tokens, 128), tokens)
 
+    def group_of(i):
+        return flip(group_me, KV_HEADS - 1 - i)
+
     def restore_group(g, _):
         cols = pl.ds(pl.multiple_of(g * HEAD_DIM, 128), HEAD_DIM)
         for part, ref in enumerate((k_ref, v_ref)):
@@ -143,7 +146,8 @@
             kv_all[g, part, own_rows, :] = (coded * wide).astype(jnp.bfloat16)
         return 0
 
-    lax.fori_loop(0, KV_HEADS, restore_group, 0)
+    for i in range(ahead):
+        restore_group(group_of(i), 0)
     doc_all[:, own_rows] = jnp.broadcast_to(doc_ref[...], (8, tokens))
     own_doc[...] = jnp.broadcast_to(doc_ref[0:1, :], (128, tokens)).T
 
@@ -172,9 +176,6 @@
 
     def landed(direction, s):
         return z >= s if direction == 0 else z <= n - 1 - s
-
-    def group_of(i):
-        return flip(group_me, KV_HEADS - 1 - i)
 
     hops = min(steps, n - 2)
     top = n - 1
@@ -326,15 +327,15 @@
     at_top, helper, below = z == top, z == top - 1, (z > 0) & (z < top - 1)
     for k in range(bits - 1):
         plan(2 * k, lambda k=k: level(0, 0, k))
-    chunk(1, 1, landed(1, 1), 1, 2, (7,))
-    chunk(0, 1, at_top, None, 0, (1, 3))
-    chunk(0, 1, helper & (z > 0), 0, 5, ())
+    chunk(1, 1, landed(1, 1), 1, 1, (5,))
+    chunk(0, 1, at_top, None, 0, (0, 1))
+    chunk(0, 1, helper & (z > 0), 0, 0, (3,))
     chunk(0, 1, below, None, 7, soon=True)
     if n > 2:
         plan(1, lambda: w_send(1, 2))
         plan(0, lambda: w_send(0, 2, helper & (z > 0)))
         plan(7, lambda: w_send(0, 2, below))
-        chunk(0, 2, at_top, None, 1, (4,), soon=True)
+        chunk(0, 2, at_top, None, 0, (2,), soon=True)
         chunk(1, 2, landed(1, 2), 7, 7, soon=True)
         chunk(0, 2, landed(0, 2) & (z < top))
     if n > 3:
@@ -375,9 +376,9 @@
 
         go(make, None, False)
         doc_copies.append(make)
-    for i in range(KV_HEADS):
+    for i in range(ahead):
         if hops:
-            kv_send(1, i, kv_room(1) if i < ahead else (z == 0) & kv_room(1))
+            kv_send(1, i, kv_room(1))
         go(lambda i=i: q_copy(i), z == top, False)
         if i == 0:
             w_send(0, 1, (z > 0) & (z < top))
@@ -386,6 +387,11 @@
             w_send(0, 1, (z == 0) & (z < top))
     for h in range(2):
         w_forward(z, h, 0, None)
+    for i in range(ahead, KV_HEADS):
+        restore_group(group_of(i), 0)
+        if hops:
+            kv_send(1, i, (z == 0) & kv_room(1))
+        go(lambda i=i: q_copy(i), z == top, False)
 
     query_at = lax.broadcasted_iota(jnp.int32, (tokens, tokens), 0)
     key_at = lax.broadcasted_iota(jnp.int32, (tokens, tokens), 1)
@@ -608,8 +614,9 @@
     reduce_block(0, 1, last_block)
     line_push(1)
     line_relay(2, 0)
+    line_relay(2, 1, helper)
     line_relay(1, 0)
-    line_relay(2, 1)
+    line_relay(2, 1, z < top - 1)
     turn(True)
     line_relay(1, 1, helper)
     if n > 3:

time: 117 us -> 111 us (0.949)
  Pallas kernels: 116 us -> 110 us
    pallas_call x1, Pallas kernels: 111 us -> 105 us  [main_step(): pl.pallas_call(functools.partial(main_kernel, bits, n, skips, 2), out_sha...]
where the time goes in v5:
time: 111 us; the launch traced here: 110 us
  Pallas kernels  110 us (99%)
    pallas_call x1, Pallas kernels, main_step(): pl.pallas_call(functools.partial(main_kernel, bits, n, skips, 2), out_sha...  105 us
    pallas_call x1, Pallas kernels, adam(): pl.pallas_call(functools.partial(adam_kernel, entries, tile), grid=(parts...  4.42 us

profile of v5, /device:TPU:0, one launch (start us, length us, event | category | flops | bytes accessed | tf_op | source)
XLA Modules:
  0.0 110.3 jit_solution(17390512550974972949)
XLA Ops:
  0.6 105.1 %shard_map.145 = (bf16[256,2304]{1,0:T(8,128)(2,1)}, f32[64,2304]{1,0:T(8,128)}, f32[8,128]{1,0:T(8,128)}) custom-call(bf16[256,2048]{1,0:T(8,128)(2,1)} %bitcast.10, bf16[256,1024]{1,0:T(8,128)(2,1)} %bitcast.11, bf16[256,1024]{1,0:T(8,128)(2,1)} %bitcast.12, s32[1,256]{1,0:T(1,128)} %doc_ref.1, bf16[256,2304]{1,0:T(8,128)(2,1)} %bitcast.9, f32[64,2304]{1,0:T(8,128)} %w_ref.3), custom_call_target="tpu_custom_call" | custom-call | tf_op jit(solution)/shard_map/pallas_call | solution.py:728
  105.7 4.4 %shard_map.146 = (f32[64,2304]{1,0:T(8,128)}, bf16[64,2304]{1,0:T(8,128)(2,1)}, f32[18,64]{1,0:T(8,128)}, bf16[64,2304]{1,0:T(8,128)(2,1)}, f32[18,64]{1,0:T(8,128)}, /*index=5*/bf16[256,2304]{1,0:T(8,128)(2,1)}) custom-call(f32[64,2304]{1,0:T(8,128)} %get-tuple-element.15.grad_ref, f32[8,128]{1,0:T(8,128)} %get-tuple-element.16.sum_ref, f32[64,2304]{1,0:T(8,128)} %w_ref.3, ...), custom_call_target="tpu_custom_call" | custom-call | tf_op jit(solution)/shard_map/pallas_call | solution.py:863
